TPU v7x, 32 devices: a whole 2x2x4 slice. The times are simulated.
32 devices in a mesh: gx: 8 (over z, x), gy: 4 (over y, core).
Axes of the slice: x: 2, y: 2, z: 4, core: 2. Of those that a mesh axis runs over, the one named last changes fastest.
Arguments:
- pressure: float32 [256, 128, 128], P('gx', 'gy'), may hold values from -6 to 6
- depth: float32 [256, 128, 128], P('gx', 'gy'), may hold values from -6 to 6
- saturation: float32 [2, 256, 128, 128], P(None, 'gx', 'gy'), may hold values from 0.05 to 0.45
- permeability: float32 [3, 256, 128, 128], P(None, 'gx', 'gy'), may hold values from 0.1 to 10
- pore_volume: float32 [256, 128, 128], P('gx', 'gy'), may hold values from 0.5 to 2
- fault_pairs: int32 [1024, 3], P(('gx', 'gy')), may hold values from 0 to 1023, as said below
- fault_kind: int32 [1024], P(('gx', 'gy')), may hold values from 0 to 15
- fault_count: int32 [32], P(('gx', 'gy')), may hold values from 8 to 32, as said below
- fault_table: float32 [16, 128], replicated, may hold values from 0.2 to 2
Outputs:
- saturation_next: float32 [3, 256, 128, 128], P(None, 'gx', 'gy')
Inputs may be any that keep to these rules, and one draw needn't show every extreme that they name: `fault_pairs`: each device holds 32 rows. Column 0 and column 2 are areal column numbers a * 32 + b of the source and target device. Column 1 is the target device i2 * 4 + j2, which lies within one index of the source device along gx and along gy, counted cyclically. Among one device's 32 rows at most 4 name the same target device, and on every device some target device is named by exactly 4 rows. Rows 0 to fault_count - 1 of a device are live; some device has 32 live rows.
All inputs are finite; a program needn't handle non-finite values.
Results may differ from a plain program's by a relative error of at most 0.0003.
Values sent between devices are 32-bit elements; how exact they have to be, the bound alone decides.
A program may use at most 64 MiB of HBM per device.

v0:
```python
import functools

import jax
import jax.numpy as jnp
from jax import lax
from jax.experimental import pallas as pl
from jax.experimental.pallas import tpu as pltpu
from jax.sharding import PartitionSpec as P

CAP = 4
ROWS = 2 * CAP
VISCOSITY = (0.5, 1.0, 0.25)
DENSITY = (1.0, 0.8, 0.25)
STEP = 0.2
MESH = pl.DeviceIdType.MESH
NEAR = [(dx, dy) for dx in (-1, 0, 1) for dy in (-1, 0, 1)]
HOME = 4
OTHERS = [n for n in range(9) if n != HOME]


def mobility(w, o):
    g = 1.0 - w - o
    return (w * w * (1.0 / VISCOSITY[0]), o * o, g * g * (1.0 / VISCOSITY[2]))


def harmonic(a, b):
    return 2.0 * a * b / (a + b)


def flux(dp, dd, low, high, trans):
    flows = []
    for f in range(3):
        drive = dp - DENSITY[f] * dd if DENSITY[f] != 1.0 else dp - dd
        flows.append(trans * jnp.where(drive > 0.0, low[f], high[f]) * drive)
    return flows


def edge_flux(low, high):
    return flux(
        low[0] - high[0],
        low[1] - high[1],
        mobility(low[2], low[3]),
        mobility(high[2], high[3]),
        harmonic(low[4], high[4]),
    )


def kernel(
    cx, cy, nz, nrow,
    p_hbm, d_hbm, s_hbm, k_hbm, v_hbm, pairs_hbm, kind_hbm, count_hbm, table_hbm,
    out,
    p, d, s, k, v, pairs_v, table, pairs_s, count_s,
    kindrow,
    idx_send, idx_recv, idx_s, send, recv, loc, back, ret,
    xhalo, yhalo, onehot,
    load_sem, own_sem, is_sem, ir_sem, smem_sem, fs_sem, fr_sem, bs_sem, br_sem,
    xs_sem, xr_sem, ys_sem, yr_sem,
):
    nx = lax.axis_size("gx")
    ny = lax.axis_size("gy")
    ix = lax.axis_index("gx")
    iy = lax.axis_index("gy")
    cells = cx * cy

    def device(dx, dy):
        return (lax.rem(ix + dx + nx, nx), lax.rem(iy + dy + ny, ny))

    loads = [
        pltpu.make_async_copy(src, dst, load_sem.at[i])
        for i, (src, dst) in enumerate(
            (
                (pairs_hbm, pairs_v),
                (kind_hbm, kindrow),
                (count_hbm, count_s),
                (table_hbm, table),
                (p_hbm, p),
                (d_hbm, d),
                (s_hbm, s),
                (k_hbm, k),
                (v_hbm, v),
            )
        )
    ]
    for c in loads:
        c.start()
    barrier = pltpu.get_barrier_semaphore()
    for n in OTHERS:
        pl.semaphore_signal(barrier, inc=1, device_id=device(*NEAR[n]), device_id_type=MESH)

    for c in loads[:4]:
        c.wait()
    lane_of_row = lax.broadcasted_iota(jnp.int32, (nrow, nrow), 1)
    sub_of_row = lax.broadcasted_iota(jnp.int32, (nrow, nrow), 0)
    eye = lane_of_row == sub_of_row
    pv = pairs_v[...]
    tgt_row = pv[1:2, :]

    def to_sublanes(row):
        return jnp.sum(jnp.where(eye, row, 0), axis=1, keepdims=True)

    src_col = to_sublanes(pv[0:1, :])
    tgt_col = to_sublanes(tgt_row)
    land_col = to_sublanes(pv[2:3, :])
    kind_col = to_sublanes(kindrow[...].reshape(1, nrow))
    rank_col = jnp.sum(
        ((tgt_col == tgt_row) & (lane_of_row < sub_of_row)).astype(jnp.int32), axis=1, keepdims=True
    )
    live_col = (lax.broadcasted_iota(jnp.int32, (nrow, 1), 0) < count_s[0]).astype(jnp.int32)
    code_col = jnp.zeros_like(tgt_col)
    for n in range(9):
        hx, hy = device(*NEAR[n])
        code_col = jnp.where(tgt_col == hx * ny + hy, n, code_col)
    lanes = lax.broadcasted_iota(jnp.int32, (nrow, 128), 1)
    message = (
        jnp.where(lanes == rank_col, land_col, 0)
        + jnp.where(lanes == CAP + rank_col, kind_col, 0)
        + jnp.where(lanes == 2 * CAP + rank_col, live_col, 0)
        + jnp.where(lanes == 3 * CAP + rank_col, src_col, 0)
    )
    for n in range(9):
        row = jnp.sum(jnp.where(code_col == n, message, 0), axis=0, keepdims=True)
        idx_send[n] = row
        if n == HOME:
            idx_recv[n] = row
    slot_col = code_col * ROWS + rank_col
    own_src = jnp.sum(jnp.where(lanes == slot_col + CAP, src_col, 0), axis=0, keepdims=True)

    pl.semaphore_wait(barrier, 8)

    def remote(src, dst, ss, rs, dev):
        return pltpu.make_async_remote_copy(
            src_ref=src, dst_ref=dst, send_sem=ss, recv_sem=rs, device_id=dev, device_id_type=MESH
        )

    idx_copies = {
        n: remote(idx_send.at[n], idx_recv.at[n], is_sem.at[n], ir_sem.at[n], device(*NEAR[n]))
        for n in OTHERS
    }
    for c in idx_copies.values():
        c.start()

    own_copy = pltpu.make_async_copy(idx_send, pairs_s, own_sem)
    own_copy.start()
    own_copy.wait()
    for c in loads[4:7]:
        c.wait()
    for n in range(9):
        dst = recv if n == HOME else send
        for r in range(CAP):
            col = pairs_s[n, 0, 3 * CAP + r]
            dst[n, r : r + 1, :nz] = p[pl.ds(col, 1), :]
            dst[n, CAP + r : CAP + r + 1, :nz] = d[pl.ds(col, 1), :]
            dst[n, r : r + 1, nz:] = s[pl.ds(col, 1), :]
            dst[n, CAP + r : CAP + r + 1, nz:] = s[pl.ds(cells + col, 1), :]
    fwd = {
        n: remote(send.at[n], recv.at[n], fs_sem.at[n], fr_sem.at[n], device(*NEAR[n]))
        for n in OTHERS
    }
    for c in fwd.values():
        c.start()

    for c in loads[7:]:
        c.wait()
    xparts = [(p, 0), (d, 0), (s, 0), (s, cells), (k, 0)]
    yparts = [(p, 0), (d, 0), (s, 0), (s, cx), (k, cx)]

    def xcopy(side, f):
        ref, base = xparts[f]
        at = base + (0 if side == 0 else cells - cy)
        return remote(
            ref.at[pl.ds(at, cy), :], xhalo.at[1 - side, f], xs_sem.at[side, f], xr_sem.at[1 - side, f],
            device(-1 if side == 0 else 1, 0),
        )

    for f in range(5):
        ref, base = yparts[f]
        base = base * cy if f >= 3 else base
        for side in range(2):
            off = base + (0 if side == 0 else cy - 1)
            yhalo[2 + side, f] = ref[pl.ds(off, cx, stride=cy), :]

    def ycopy(side):
        return remote(
            yhalo.at[2 + side], yhalo.at[1 - side], ys_sem.at[side], yr_sem.at[1 - side],
            device(0, -1 if side == 0 else 1),
        )

    has = ((ix > 0, ix < nx - 1), (iy > 0, iy < ny - 1))
    for side in range(2):
        @pl.when(has[0][side])
        def _():
            for f in range(5):
                xcopy(side, f).start()

        @pl.when(has[1][side])
        def _():
            ycopy(side).start()

    zmask = lax.broadcasted_iota(jnp.int32, (cy, nz), 1) < nz - 1
    ymask = lax.broadcasted_iota(jnp.int32, (cy, nz), 0) < cy - 1

    def slab(a, carry):
        base = pl.multiple_of(a * cy, cy)
        after = pl.multiple_of(jnp.minimum(a + 1, cx - 1) * cy, cy)

        def at(ref, off):
            return ref[pl.ds(off, cy), :]

        p0, d0 = at(p, base), at(d, base)
        w0, o0 = at(s, base), at(s, cells + base)
        m0 = mobility(w0, o0)
        m1 = mobility(at(s, after), at(s, cells + after))
        tx = jnp.where(a < cx - 1, harmonic(at(k, base), at(k, after)), 0.0)
        fx = flux(p0 - at(p, after), d0 - at(d, after), m0, m1, tx)
        net = [fx[f] - carry[f] for f in range(3)]
        for axis, size, mask, offset in ((0, cy, ymask, cells), (1, nz, zmask, 2 * cells)):
            def up(x):
                return pltpu.roll(x, size - 1, axis)

            kk = at(k, offset + base)
            t = jnp.where(mask, harmonic(kk, up(kk)), 0.0)
            fl = flux(p0 - up(p0), d0 - up(d0), m0, [up(m) for m in m0], t)
            net = [net[f] + (fl[f] - pltpu.roll(fl[f], 1, axis)) for f in range(3)]
        scale = STEP / at(v, base)
        v[pl.ds(base, cy), :] = scale
        now = (w0, o0, 1.0 - w0 - o0)
        for f in range(3):
            out[pl.ds(f * cells + base, cy), :] = now[f] - scale * net[f]
        return tuple(fx)

    zero = jnp.zeros((cy, nz), jnp.float32)
    half = cx // 2
    carry = lax.fori_loop(0, half, slab, (zero, zero, zero), unroll=2)

    for c in idx_copies.values():
        c.wait()
    to_smem = pltpu.make_async_copy(idx_recv, idx_s, smem_sem)
    to_smem.start()
    lane1 = lax.broadcasted_iota(jnp.int32, (1, 128), 1)
    spot = own_src
    for n in range(9):
        row = jnp.where(lane1 < CAP, idx_recv[n], 0)
        spot = spot + (pltpu.roll(row, n * ROWS, 1) if n else row)
    to_smem.wait()
    for n in range(9):
        for r in range(CAP):
            land = idx_s[n, 0, r]
            kd = idx_s[n, 0, CAP + r]
            live = idx_s[n, 0, 2 * CAP + r].astype(jnp.float32)
            at = n * ROWS + r
            loc[0, pl.ds(at, 1), :] = p[pl.ds(land, 1), :]
            loc[1, pl.ds(at, 1), :] = d[pl.ds(land, 1), :]
            loc[2, pl.ds(at, 1), :] = s[pl.ds(land, 1), :]
            loc[3, pl.ds(at, 1), :] = s[pl.ds(cells + land, 1), :]
            loc[4, pl.ds(at, 1), :] = table[pl.ds(kd, 1), :] * live
    for c in fwd.values():
        c.wait()
    top = lax.broadcasted_iota(jnp.int32, (ROWS, nz), 0) < CAP
    landed = []
    for n in range(9):
        first = recv[n]
        second = pltpu.roll(first, CAP, 0)
        rows = pl.ds(n * ROWS, ROWS)
        fl = flux(
            first[:, :nz] - loc[0, rows, :],
            second[:, :nz] - loc[1, rows, :],
            mobility(first[:, nz:], second[:, nz:]),
            mobility(loc[2, rows, :], loc[3, rows, :]),
            loc[4, rows, :],
        )
        fl = [jnp.where(top, x, 0.0) for x in fl]
        for f in range(3):
            (ret if n == HOME else back)[n, :, f * nz : (f + 1) * nz] = fl[f]
    rev = {
        n: remote(back.at[n], ret.at[n], bs_sem.at[n], br_sem.at[n], device(-NEAR[n][0], -NEAR[n][1]))
        for n in OTHERS
    }
    for c in rev.values():
        c.start()
    slots = 9 * ROWS
    kl = 3 * slots
    wide = jnp.concatenate([spot, jnp.zeros_like(spot)], axis=1)
    spot = wide + pltpu.roll(wide, slots, 1) + pltpu.roll(wide, 2 * slots, 1)
    for c in range(cx):
        ids = lax.broadcasted_iota(jnp.int32, (cy, kl), 0) + c * cy
        onehot[c * cy : (c + 1) * cy, :] = (ids == spot[:, :kl]).astype(jnp.float32).astype(jnp.bfloat16)

    lax.fori_loop(half, cx, slab, carry, unroll=2)

    for side in range(2):
        @pl.when(has[0][side])
        def _():
            for f in range(5):
                xcopy(side, f).wait_send()
                xcopy(1 - side, f).wait_recv()
            at = 0 if side == 0 else cells - cy
            mine = [ref[pl.ds(base + at, cy), :] for ref, base in xparts]
            near = [xhalo[side, f] for f in range(5)]
            low, high = (near, mine) if side == 0 else (mine, near)
            fl = edge_flux(low, high)
            scale = v[pl.ds(at, cy), :]
            for f in range(3):
                rows = pl.ds(f * cells + at, cy)
                out[rows, :] = out[rows, :] + (scale * fl[f] if side == 0 else -scale * fl[f])

    for side in range(2):
        @pl.when(has[1][side])
        def _():
            ycopy(side).wait_send()
            ycopy(1 - side).wait_recv()
            at = 0 if side == 0 else cy - 1
            mine = [yhalo[2 + side, f] for f in range(5)]
            near = [yhalo[side, f] for f in range(5)]
            low, high = (near, mine) if side == 0 else (mine, near)
            fl = edge_flux(low, high)
            scale = v[pl.ds(at, cx, stride=cy), :]
            for f in range(3):
                rows = pl.ds(f * cells + at, cx, stride=cy)
                out[rows, :] = out[rows, :] + (scale * fl[f] if side == 0 else -scale * fl[f])

    for c in rev.values():
        c.wait()
    rows = []
    for n in range(9):
        own = ret[n]
        here = ret[n] if n == HOME else back[n]
        rows.append(pltpu.roll(own, CAP, 0) - here)
    flows = jnp.concatenate(rows, axis=0)
    hi = flows.astype(jnp.bfloat16).astype(jnp.float32)
    rest = flows - hi
    mid = rest.astype(jnp.bfloat16).astype(jnp.float32)
    parts = jnp.concatenate([hi, mid, rest - mid], axis=0).astype(jnp.bfloat16)
    step = 8 * cy
    for c in range(cells // step):
        hot = onehot[c * step : (c + 1) * step, :]
        add = jnp.dot(hot, parts, preferred_element_type=jnp.float32)
        scale = v[c * step : (c + 1) * step, :]
        for f in range(3):
            at = pl.ds(f * cells + c * step, step)
            out[at, :] = out[at, :] - scale * add[:, f * nz : (f + 1) * nz]


def body(pressure, depth, saturation, permeability, pore_volume, pairs, kind, count, table):
    cx, cy, nz = pressure.shape
    nrow = pairs.shape[0]
    kinds = table.shape[0]
    cells = cx * cy
    f32 = jnp.float32
    dma = pltpu.SemaphoreType.DMA
    any_spec = pl.BlockSpec(memory_space=pltpu.HBM)
    out = pl.pallas_call(
        functools.partial(kernel, cx, cy, nz, nrow),
        out_shape=pltpu.VMEM((3 * cells, nz), f32),
        in_specs=[any_spec] * 9,
        out_specs=pl.BlockSpec(memory_space=pltpu.VMEM),
        scratch_shapes=[
            pltpu.VMEM((cells, nz), f32),
            pltpu.VMEM((cells, nz), f32),
            pltpu.VMEM((2 * cells, nz), f32),
            pltpu.VMEM((3 * cells, nz), f32),
            pltpu.VMEM((cells, nz), f32),
            pltpu.VMEM((3, nrow), jnp.int32),
            pltpu.VMEM((kinds, nz), f32),
            pltpu.SMEM((9, 1, 128), jnp.int32),
            pltpu.SMEM((1,), jnp.int32),
            pltpu.VMEM((nrow,), jnp.int32),
            pltpu.VMEM((9, 1, 128), jnp.int32),
            pltpu.VMEM((9, 1, 128), jnp.int32),
            pltpu.SMEM((9, 1, 128), jnp.int32),
            pltpu.VMEM((9, ROWS, 2 * nz), f32),
            pltpu.VMEM((9, ROWS, 2 * nz), f32),
            pltpu.VMEM((5, 9 * ROWS, nz), f32),
            pltpu.VMEM((9, ROWS, 3 * nz), f32),
            pltpu.VMEM((9, ROWS, 3 * nz), f32),
            pltpu.VMEM((2, 5, cy, nz), f32),
            pltpu.VMEM((4, 5, cx, nz), f32),
            pltpu.VMEM((cells, 27 * ROWS), jnp.bfloat16),
            dma((9,)), dma,
            dma((9,)), dma((9,)), dma,
            dma((9,)), dma((9,)), dma((9,)), dma((9,)),
            dma((2, 5)), dma((2, 5)), dma((2,)), dma((2,)),
        ],
        compiler_params=pltpu.CompilerParams(
            collective_id=0, has_side_effects=True, vmem_limit_bytes=60000000
        ),
    )(
        pressure.reshape(cells, nz),
        depth.reshape(cells, nz),
        saturation.reshape(2 * cells, nz),
        permeability.reshape(3 * cells, nz),
        pore_volume.reshape(cells, nz),
        pairs.T,
        kind,
        count,
        table,
    )
    return out.reshape(3, cx, cy, nz)


def solution(mesh):
    cell = P("gx", "gy", None)
    cells = P(None, "gx", "gy", None)
    both = ("gx", "gy")
    return jax.shard_map(
        body,
        mesh=mesh,
        in_specs=(cell, cell, cells, cells, cell, P(both, None), P(both), P(both), P()),
        out_specs=cells,
        check_vma=False,
    )
```

profile of v0, /device:TPU:1, one launch (start us, length us, event | category | flops | bytes accessed | tf_op | source)
XLA Modules:
  0.0 19.2 jit_solution(669760919226399039)
XLA Ops:
  0.7 17.4 %shard_map.91 = f32[3072,128]{1,0:T(8,128)S(1)} custom-call(f32[1024,128]{1,0:T(8,128)} %bitcast.10, f32[1024,128]{1,0:T(8,128)} %bitcast.11, f32[2048,128]{1,0:T(8,128)} %bitcast.9, f32[3072,128]{1,0:T(8,128)} %bitcast.8, f32[1024,128]{1,0:T(8,128)} %bitcast.12, s32[3,32]{1,0:T(4,128)} %bitcast.13, s32[32]{0:T(128)} %kind_hbm.1, s32[1]{0:T(128)S(6)} %copy.12.count_hbm, ...), custom_call_target="tpu_custom_call" | custom-call | tf_op jit(solution)/shard_map/pallas_call | solution.py:351
  18.1 1.1 %copy.11 = f32[3,32,32,128]{3,2,1,0:T(8,128)} copy(f32[3,32,32,128]{3,2,1,0:T(8,128)S(1)} %bitcast.7) | data formatting | bytes 3145728
where the time goes:
time: 19.4 us; the launch traced here: 19.2 us
  Pallas kernels  17.4 us (90%)
  local copies, waits for them, and re-layouts  1.15 us (6%)
  between operations  0.66 us (3%)
    pallas_call x1, Pallas kernels, body(): pl.pallas_call(functools.partial(kernel, cx, cy, nz, nrow), out_shape=plt...  17.4 us
    unnamed x1, local copies, waits for them, and re-layouts  1.15 us

commit v1 on v0

v1 whole, which is shorter than its diff:
```python
import functools

import jax
import jax.numpy as jnp
from jax import lax
from jax.experimental import pallas as pl
from jax.experimental.pallas import tpu as pltpu
from jax.sharding import PartitionSpec as P

CAP = 4
ROWS = 2 * CAP
VISCOSITY = (0.5, 1.0, 0.25)
DENSITY = (1.0, 0.8, 0.25)
STEP = 0.2
MESH = pl.DeviceIdType.MESH
NEAR = [(dx, dy) for dx in (-1, 0, 1) for dy in (-1, 0, 1)]
HOME = 4
OTHERS = [n for n in range(9) if n != HOME]
PIECES = 12


def mobility(w, o):
    g = 1.0 - w - o
    return (w * w * (1.0 / VISCOSITY[0]), o * o, g * g * (1.0 / VISCOSITY[2]))


def harmonic(a, b):
    return 2.0 * a * b / (a + b)


def flux(dp, dd, low, high, trans):
    flows = []
    for f in range(3):
        drive = dp - DENSITY[f] * dd if DENSITY[f] != 1.0 else dp - dd
        flows.append(trans * jnp.where(drive > 0.0, low[f], high[f]) * drive)
    return flows


def edge_flux(low, high):
    return flux(
        low[0] - high[0],
        low[1] - high[1],
        mobility(low[2], low[3]),
        mobility(high[2], high[3]),
        harmonic(low[4], high[4]),
    )


def kernel(
    cx, cy, nz, nrow,
    p_hbm, d_hbm, s_hbm, k_hbm, v_hbm, pairs_hbm, kind_hbm, count_hbm, table_hbm,
    out, res, own_s,
    cell, k, v, table, pairs_v, count_s, kindrow,
    idx_send, idx_s, send, recv, loc, tloc, back, ret, scl,
    xhalo, yhalo,
    load_sem, own_sem, is_sem, ir_sem, fs_sem, fr_sem, bs_sem, br_sem,
    xs_sem, xr_sem, ys_sem, yr_sem,
):
    nx = lax.axis_size("gx")
    ny = lax.axis_size("gy")
    ix = lax.axis_index("gx")
    iy = lax.axis_index("gy")
    cells = cx * cy
    p, d, s = (cell.at[pl.ds(i * cells, (1, 1, 2)[i] * cells)] for i in range(3))

    def device(dx, dy):
        return (lax.rem(ix + dx + nx, nx), lax.rem(iy + dy + ny, ny))

    def remote(src, dst, ss, rs, dev):
        return pltpu.make_async_remote_copy(
            src_ref=src, dst_ref=dst, send_sem=ss, recv_sem=rs, device_id=dev, device_id_type=MESH
        )

    def arrived(ref, sem):
        pltpu.make_async_copy(ref, ref, sem).wait()

    barrier = pltpu.get_barrier_semaphore()
    for n in OTHERS:
        pl.semaphore_signal(barrier, inc=1, device_id=device(*NEAR[n]), device_id_type=MESH)
    loads = [
        pltpu.make_async_copy(src, dst, load_sem.at[i])
        for i, src, dst in (
            (0, pairs_hbm, pairs_v),
            (1, kind_hbm, kindrow),
            (2, count_hbm, count_s),
            (3, p_hbm, p),
            (3, d_hbm, d),
            (3, s_hbm, s),
            (4, k_hbm, k),
            (5, v_hbm, v),
            (6, table_hbm, table),
        )
    ]
    for c in loads:
        c.start()

    for c in loads[:3]:
        c.wait()
    lane_of_row = lax.broadcasted_iota(jnp.int32, (nrow, nrow), 1)
    sub_of_row = lax.broadcasted_iota(jnp.int32, (nrow, nrow), 0)
    eye = lane_of_row == sub_of_row
    pv = pairs_v[...]
    tgt_row = pv[1:2, :]

    def to_sublanes(row):
        return jnp.sum(jnp.where(eye, row, 0), axis=1, keepdims=True)

    src_col = to_sublanes(pv[0:1, :])
    tgt_col = to_sublanes(tgt_row)
    land_col = to_sublanes(pv[2:3, :])
    kind_col = to_sublanes(kindrow[...].reshape(1, nrow))
    rank_col = jnp.sum(
        ((tgt_col == tgt_row) & (lane_of_row < sub_of_row)).astype(jnp.int32), axis=1, keepdims=True
    )
    live_col = (lax.broadcasted_iota(jnp.int32, (nrow, 1), 0) < count_s[0]).astype(jnp.int32)
    code_col = jnp.zeros_like(tgt_col)
    for n in range(9):
        hx, hy = device(*NEAR[n])
        code_col = jnp.where(tgt_col == hx * ny + hy, n, code_col)
    lanes = lax.broadcasted_iota(jnp.int32, (nrow, 128), 1)
    message = (
        jnp.where(lanes == rank_col, land_col, 0)
        + jnp.where(lanes == CAP + rank_col, kind_col, 0)
        + jnp.where(lanes == 2 * CAP + rank_col, live_col, 0)
        + jnp.where(lanes == 3 * CAP + rank_col, src_col, 0)
    )
    for n in range(9):
        idx_send[n] = jnp.sum(jnp.where(code_col == n, message, 0), axis=0, keepdims=True)

    own_copy = pltpu.make_async_copy(idx_send, own_s, own_sem)
    own_copy.start()
    arrived(cell, load_sem.at[3])
    own_copy.wait()
    for n in range(9):
        dst = recv if n == HOME else send
        for r in range(CAP):
            col = own_s[n, 0, 3 * CAP + r]
            dst[n, r : r + 1, :nz] = p[pl.ds(col, 1), :]
            dst[n, CAP + r : CAP + r + 1, :nz] = d[pl.ds(col, 1), :]
            dst[n, r : r + 1, nz:] = s[pl.ds(col, 1), :]
            dst[n, CAP + r : CAP + r + 1, nz:] = s[pl.ds(cells + col, 1), :]

    odd = lax.rem(ix, 2)
    away = 2 * odd - 1

    def ask(dx, dy):
        n = 3 * (dx + 1) + dy + 1
        dev = device(dx, dy)
        remote(idx_send.at[n], idx_s.at[n], is_sem, ir_sem.at[dx + 1], dev).start()
        remote(send.at[n], recv.at[n], fs_sem, fr_sem.at[dx + 1], dev).start()

    pl.semaphore_wait(barrier, 8)
    for dx in (away, -away):
        for dy in (-1, 1, 0):
            ask(dx, dy)
    for dy in (-1, 1):
        ask(0, dy)

    for c in loads[6:]:
        c.wait()
    xparts = [(p, 0), (d, 0), (s, 0), (s, cells), (k, 0)]
    yparts = [(p, 0), (d, 0), (s, 0), (s, cx), (k, cx)]

    def xcopy(side, f):
        ref, base = xparts[f]
        at = base + (0 if side == 0 else cells - cy)
        return remote(
            ref.at[pl.ds(at, cy), :], xhalo.at[1 - side, f], xs_sem.at[side], xr_sem.at[1 - side],
            device(-1 if side == 0 else 1, 0),
        )

    for f in range(5):
        ref, base = yparts[f]
        base = base * cy if f >= 3 else base
        for side in range(2):
            off = base + (0 if side == 0 else cy - 1)
            yhalo[2 + side, f] = ref[pl.ds(off, cx, stride=cy), :]

    def ycopy(side):
        return remote(
            yhalo.at[2 + side], yhalo.at[1 - side], ys_sem.at[side], yr_sem.at[1 - side],
            device(0, -1 if side == 0 else 1),
        )

    has = ((ix > 0, ix < nx - 1), (iy > 0, iy < ny - 1))
    for side in range(2):
        @pl.when(has[0][side])
        def _():
            for f in range(5):
                xcopy(side, f).start()

        @pl.when(has[1][side])
        def _():
            ycopy(side).start()

    zmask = lax.broadcasted_iota(jnp.int32, (cy, nz), 1) < nz - 1
    ymask = lax.broadcasted_iota(jnp.int32, (cy, nz), 0) < cy - 1

    def slab(a, carry):
        base = pl.multiple_of(a * cy, cy)
        after = pl.multiple_of(jnp.minimum(a + 1, cx - 1) * cy, cy)

        def at(ref, off):
            return ref[pl.ds(off, cy), :]

        p0, d0 = at(p, base), at(d, base)
        w0, o0 = at(s, base), at(s, cells + base)
        m0 = mobility(w0, o0)
        m1 = mobility(at(s, after), at(s, cells + after))
        tx = jnp.where(a < cx - 1, harmonic(at(k, base), at(k, after)), 0.0)
        fx = flux(p0 - at(p, after), d0 - at(d, after), m0, m1, tx)
        net = [fx[f] - carry[f] for f in range(3)]
        for axis, size, mask, offset in ((0, cy, ymask, cells), (1, nz, zmask, 2 * cells)):
            def up(x):
                return pltpu.roll(x, size - 1, axis)

            kk = at(k, offset + base)
            t = jnp.where(mask, harmonic(kk, up(kk)), 0.0)
            fl = flux(p0 - up(p0), d0 - up(d0), m0, [up(m) for m in m0], t)
            net = [net[f] + (fl[f] - pltpu.roll(fl[f], 1, axis)) for f in range(3)]
        scale = STEP / at(v, base)
        v[pl.ds(base, cy), :] = scale
        now = (w0, o0, 1.0 - w0 - o0)
        for f in range(3):
            out[pl.ds(f * cells + base, cy), :] = now[f] - scale * net[f]
        return tuple(fx)

    zero = jnp.zeros((cy, nz), jnp.float32)
    lax.fori_loop(0, cx, slab, (zero, zero, zero), unroll=2)

    def answer(group, sources):
        first = 3 * group
        for i, ints in enumerate(sources):
            n = first + i
            for r in range(CAP):
                land = ints[n, 0, r]
                kd = ints[n, 0, CAP + r]
                live = ints[n, 0, 2 * CAP + r].astype(jnp.float32)
                loc[n, r : r + 1, :nz] = p[pl.ds(land, 1), :]
                loc[n, CAP + r : CAP + r + 1, :nz] = d[pl.ds(land, 1), :]
                loc[n, r : r + 1, nz:] = s[pl.ds(land, 1), :]
                loc[n, CAP + r : CAP + r + 1, nz:] = s[pl.ds(cells + land, 1), :]
                tloc[n, r : r + 1, :] = table[pl.ds(kd, 1), :] * live

    def flows_of(group):
        rows = pl.ds(3 * group, 3)
        far, here = recv[rows], loc[rows]

        def second(x):
            return pltpu.roll(x, CAP, 1)

        gap = far[:, :, :nz] - here[:, :, :nz]
        fl = flux(
            gap,
            second(gap),
            mobility(far[:, :, nz:], second(far[:, :, nz:])),
            mobility(here[:, :, nz:], second(here[:, :, nz:])),
            tloc[rows],
        )
        for f in range(3):
            back[rows, :, f * nz : (f + 1) * nz] = fl[f][:, :CAP]

    def reply(dx, dy):
        n = 3 * (dx + 1) + dy + 1
        return remote(back.at[n], ret.at[n], bs_sem, br_sem, device(-dx, -dy))

    for dx in (0, away, -away):
        group = dx + 1
        still = isinstance(dx, int)
        many = 2 if still else 3
        arrived(idx_s.at[pl.ds(3 * group, many)], ir_sem.at[group])
        answer(group, (idx_s, own_s, idx_s) if still else (idx_s,) * 3)
        arrived(recv.at[pl.ds(3 * group, many)], fr_sem.at[group])
        flows_of(group)
        for dy in (-1, 1) if still else (-1, 1, 0):
            reply(dx, dy).start()

    for side in range(2):
        @pl.when(has[0][side])
        def _():
            arrived(xhalo.at[side], xs_sem.at[side])
            arrived(xhalo.at[side], xr_sem.at[side])
            at = 0 if side == 0 else cells - cy
            mine = [ref[pl.ds(base + at, cy), :] for ref, base in xparts]
            near = [xhalo[side, f] for f in range(5)]
            low, high = (near, mine) if side == 0 else (mine, near)
            fl = edge_flux(low, high)
            scale = v[pl.ds(at, cy), :]
            for f in range(3):
                rows = pl.ds(f * cells + at, cy)
                out[rows, :] = out[rows, :] + (scale * fl[f] if side == 0 else -scale * fl[f])

    for side in range(2):
        @pl.when(has[1][side])
        def _():
            ycopy(side).wait_send()
            ycopy(1 - side).wait_recv()
            at = 0 if side == 0 else cy - 1
            mine = [yhalo[2 + side, f] for f in range(5)]
            near = [yhalo[side, f] for f in range(5)]
            low, high = (near, mine) if side == 0 else (mine, near)
            fl = edge_flux(low, high)
            scale = v[pl.ds(at, cx, stride=cy), :]
            for f in range(3):
                rows = pl.ds(f * cells + at, cx, stride=cy)
                out[rows, :] = out[rows, :] + (scale * fl[f] if side == 0 else -scale * fl[f])

    lane1 = lax.broadcasted_iota(jnp.int32, (1, 128), 1)
    slots = 10 * CAP
    spot = jnp.full((1, 128), -1, jnp.int32)
    for n in range(9):
        for r in range(CAP):
            spot = jnp.where(lane1 == n * CAP + r, (own_s if n == HOME else idx_s)[n, 0, r], spot)
    for r in range(CAP):
        spot = jnp.where(lane1 == 9 * CAP + r, own_s[HOME, 0, 3 * CAP + r], spot)
    spot = jnp.where(lane1 < slots, spot, 0)
    spot = spot + pltpu.roll(spot, slots, 1) + pltpu.roll(spot, 2 * slots, 1)
    flows = jnp.concatenate([-back[n] for n in range(9)] + [back[HOME]], axis=0)
    hi = flows.astype(jnp.bfloat16).astype(jnp.float32)
    rest = flows - hi
    mid = rest.astype(jnp.bfloat16).astype(jnp.float32)
    pad = jnp.zeros((128 - 3 * slots, 3 * nz), jnp.float32)
    parts = jnp.concatenate([hi, mid, rest - mid, pad], axis=0).astype(jnp.bfloat16)
    step = 8 * cy
    for c in range(cells // step):
        ids = lax.broadcasted_iota(jnp.int32, (step, 128), 0) + c * step
        hot = (ids == spot).astype(jnp.float32).astype(jnp.bfloat16)
        add = jnp.dot(hot, parts, preferred_element_type=jnp.float32)
        scale = v[c * step : (c + 1) * step, :]
        for f in range(3):
            at = pl.ds(f * cells + c * step, step)
            out[at, :] = out[at, :] - scale * add[:, f * nz : (f + 1) * nz]

    for n in OTHERS:
        for r in range(CAP):
            scl[n, r : r + 1, :] = v[pl.ds(own_s[n, 0, 3 * CAP + r], 1), :]
    arrived(idx_send.at[pl.ds(0, 8)], is_sem)
    arrived(send.at[pl.ds(0, 8)], fs_sem)
    arrived(back.at[pl.ds(0, 8)], bs_sem)
    arrived(ret.at[pl.ds(0, 8)], br_sem)
    for n in OTHERS:
        for f in range(3):
            res[n, :, f * nz : (f + 1) * nz] = ret[n, :, f * nz : (f + 1) * nz] * scl[n]


def finish(cells, nz, part, res_in, own_s, held, res, final, sem):
    for n in OTHERS:
        for r in range(CAP):
            col = own_s[n, 0, 3 * CAP + r]
            for f in range(3):
                row = pl.ds(f * cells + col, 1)
                held[row, :] = held[row, :] - res[n, r : r + 1, f * nz : (f + 1) * nz]
    size = 3 * cells // PIECES
    for i in range(PIECES):
        rows = pl.ds(i * size, size)
        pltpu.make_async_copy(held.at[rows], final.at[rows], sem).start()
    pltpu.make_async_copy(held, final, sem).wait()


def body(pressure, depth, saturation, permeability, pore_volume, pairs, kind, count, table):
    cx, cy, nz = pressure.shape
    nrow = pairs.shape[0]
    kinds = table.shape[0]
    cells = cx * cy
    f32 = jnp.float32
    dma = pltpu.SemaphoreType.DMA
    any_spec = pl.BlockSpec(memory_space=pltpu.HBM)
    vmem = pl.BlockSpec(memory_space=pltpu.VMEM)
    smem = pl.BlockSpec(memory_space=pltpu.SMEM)
    part, res, own = pl.pallas_call(
        functools.partial(kernel, cx, cy, nz, nrow),
        out_shape=(
            pltpu.VMEM((3 * cells, nz), f32),
            pltpu.VMEM((9, CAP, 3 * nz), f32),
            pltpu.SMEM((9, 1, 128), jnp.int32),
        ),
        in_specs=[any_spec] * 9,
        out_specs=(vmem, vmem, smem),
        scratch_shapes=[
            pltpu.VMEM((4 * cells, nz), f32),
            pltpu.VMEM((3 * cells, nz), f32),
            pltpu.VMEM((cells, nz), f32),
            pltpu.VMEM((kinds, nz), f32),
            pltpu.VMEM((3, nrow), jnp.int32),
            pltpu.SMEM((1,), jnp.int32),
            pltpu.VMEM((nrow,), jnp.int32),
            pltpu.VMEM((9, 1, 128), jnp.int32),
            pltpu.SMEM((9, 1, 128), jnp.int32),
            pltpu.VMEM((9, ROWS, 2 * nz), f32),
            pltpu.VMEM((9, ROWS, 2 * nz), f32),
            pltpu.VMEM((9, ROWS, 2 * nz), f32),
            pltpu.VMEM((9, ROWS, nz), f32),
            pltpu.VMEM((9, CAP, 3 * nz), f32),
            pltpu.VMEM((9, CAP, 3 * nz), f32),
            pltpu.VMEM((9, CAP, nz), f32),
            pltpu.VMEM((2, 5, cy, nz), f32),
            pltpu.VMEM((4, 5, cx, nz), f32),
            dma((7,)), dma,
            dma, dma((3,)), dma, dma((3,)), dma, dma,
            dma((2,)), dma((2,)), dma((2,)), dma((2,)),
        ],
        compiler_params=pltpu.CompilerParams(
            collective_id=0, has_side_effects=True, vmem_limit_bytes=60000000
        ),
    )(
        pressure.reshape(cells, nz),
        depth.reshape(cells, nz),
        saturation.reshape(2 * cells, nz),
        permeability.reshape(3 * cells, nz),
        pore_volume.reshape(cells, nz),
        pairs.T,
        kind,
        count,
        table,
    )
    _, _, out = pl.pallas_call(
        functools.partial(finish, cells, nz),
        out_shape=(
            pltpu.VMEM((3 * cells, nz), f32),
            pltpu.VMEM((9, CAP, 3 * nz), f32),
            jax.ShapeDtypeStruct((3 * cells, nz), f32),
        ),
        in_specs=[vmem, vmem, smem],
        out_specs=(vmem, vmem, any_spec),
        scratch_shapes=[dma],
        input_output_aliases={0: 0, 1: 1},
    )(part, res, own)
    return out.reshape(3, cx, cy, nz)


def solution(mesh):
    cell = P("gx", "gy", None)
    cells = P(None, "gx", "gy", None)
    both = ("gx", "gy")
    return jax.shard_map(
        body,
        mesh=mesh,
        in_specs=(cell, cell, cells, cells, cell, P(both, None), P(both), P(both), P()),
        out_specs=cells,
        check_vma=False,
    )
```

time: 19.4 us -> 17.5 us (0.902)
  the two profiles are of different devices: /device:TPU:1 before, /device:TPU:0 now
where the time goes in v1:
time: 17.5 us; the launch traced here: 17.3 us
  Pallas kernels  16.7 us (95%)
  between operations  0.66 us (4%)
    pallas_call x1, Pallas kernels, body(): pl.pallas_call(functools.partial(kernel, cx, cy, nz, nrow), out_shape=(pl...  15.4 us
    pallas_call x1, Pallas kernels, body(): pl.pallas_call(functools.partial(finish, cells, nz), out_shape=(pltpu.VME...  1.29 us

profile of v1, /device:TPU:0, one launch (start us, length us, event | category | flops | bytes accessed | tf_op | source)
XLA Modules:
  0.0 17.3 jit_solution(10889393307509539049)
XLA Ops:
  0.7 15.4 %shard_map.91 = (f32[3072,128]{1,0:T(8,128)S(1)}, f32[9,4,384]{2,1,0:T(4,128)S(1)}, s32[9,1,128]{2,1,0:T(1,128)S(4)}) custom-call(f32[1024,128]{1,0:T(8,128)} %bitcast.9, f32[1024,128]{1,0:T(8,128)} %bitcast.10, f32[2048,128]{1,0:T(8,128)} %bitcast.8, f32[3072,128]{1,0:T(8,128)} %bitcast.7, f32[1024,128]{1,0:T(8,128)} %bitcast.11, s32[3,32]{1,0:T(4,128)} %bitcast.12, ...), custom_call_target="tpu_custom_call" | custom-call | tf_op jit(solution)/shard_map/pallas_call | solution.py:370
  16.0 1.3 %shard_map.92 = (f32[3072,128]{1,0:T(8,128)S(1)}, f32[9,4,384]{2,1,0:T(4,128)S(1)}, f32[3072,128]{1,0:T(8,128)}) custom-call(f32[3072,128]{1,0:T(8,128)S(1)} %get-tuple-element.9.part, f32[9,4,384]{2,1,0:T(4,128)S(1)} %get-tuple-element.10.res_in, s32[9,1,128]{2,1,0:T(1,128)S(4)} %get-tuple-element.11.own_s), custom_call_target="tpu_custom_call", output_to_operand_aliasing={{0}: (0, {}), {1}: (1, {})} | custom-call | tf_op jit(solution)/shard_map/pallas_call | solution.py:416

commit v2 on v1

--- a/solution.py
+++ b/solution.py
@@ -55,6 +55,7 @@
     xhalo, yhalo,
     load_sem, own_sem, is_sem, ir_sem, fs_sem, fr_sem, bs_sem, br_sem,
     xs_sem, xr_sem, ys_sem, yr_sem,
+    between, via_i, via_f, vi_sem, vf_sem, ws_sem, go_sem, here_sem,
 ):
     nx = lax.axis_size("gx")
     ny = lax.axis_size("gy")
@@ -74,9 +75,35 @@
     def arrived(ref, sem):
         pltpu.make_async_copy(ref, ref, sem).wait()
 
+    def signal(sem, dev):
+        pl.semaphore_signal(sem, inc=1, device_id=dev, device_id_type=MESH)
+
+    def wrap(y):
+        return lax.rem(y + 2 * ny, ny)
+
+    first, last = ix == 0, ix == nx - 1
+    y_odd = lax.rem(iy, 2)
+    relays = (ix == 1) & (y_odd == 1)
     barrier = pltpu.get_barrier_semaphore()
     for n in OTHERS:
-        pl.semaphore_signal(barrier, inc=1, device_id=device(*NEAR[n]), device_id_type=MESH)
+        dx, dy = NEAR[n]
+        if dx == 1:
+            @pl.when(ix < nx - 2)
+            def _():
+                signal(barrier, device(dx, dy))
+        elif dx == 0:
+            @pl.when(~last)
+            def _():
+                signal(barrier, device(dx, dy))
+        else:
+            signal(barrier, device(dx, dy))
+
+    @pl.when(relays)
+    def _():
+        signal(barrier, (nx - 1, wrap(iy - 1)))
+        signal(barrier, (nx - 1, iy))
+        signal(barrier, (0, wrap(iy - 2)))
+
     loads = [
         pltpu.make_async_copy(src, dst, load_sem.at[i])
         for i, src, dst in (
@@ -93,6 +120,13 @@
     ]
     for c in loads:
         c.start()
+
+    @pl.when(last)
+    def _():
+        pl.semaphore_wait(barrier, 4)
+        signal(go_sem.at[y_odd], (1, iy + 1 - y_odd))
+        for dy in (-1, 0, 1):
+            signal(here_sem, (0, wrap(iy + dy)))
 
     for c in loads[:3]:
         c.wait()
@@ -149,10 +183,37 @@
         remote(idx_send.at[n], idx_s.at[n], is_sem, ir_sem.at[dx + 1], dev).start()
         remote(send.at[n], recv.at[n], fs_sem, fr_sem.at[dx + 1], dev).start()
 
-    pl.semaphore_wait(barrier, 8)
-    for dx in (away, -away):
+    @pl.when(first)
+    def _():
+        pl.semaphore_wait(barrier, 5 + y_odd)
+        for dy in (-1, 0, 1):
+            ty = wrap(iy + dy)
+            t_odd = lax.rem(ty, 2)
+            slot = 3 * t_odd + dy + 1
+            via = (1, ty + 1 - t_odd)
+            remote(idx_send.at[dy + 1], via_i.at[slot], is_sem, vi_sem.at[t_odd], via).start()
+            remote(send.at[dy + 1], via_f.at[slot], fs_sem, vf_sem.at[t_odd], via).start()
+
+    @pl.when(~first)
+    def _():
+        @pl.when(~last)
+        def _():
+            pl.semaphore_wait(barrier, 8)
+
+        @pl.when(ix == nx - 2)
+        def _():
+            for dy in (-1, 0, 1):
+                signal(here_sem, device(1, dy))
+
+        @pl.when(last)
+        def _():
+            pl.semaphore_wait(here_sem, 3)
+
         for dy in (-1, 1, 0):
-            ask(dx, dy)
+            ask(away, dy)
+
+    for dy in (-1, 1, 0):
+        ask(-away, dy)
     for dy in (-1, 1):
         ask(0, dy)
 
@@ -181,17 +242,6 @@
             yhalo.at[2 + side], yhalo.at[1 - side], ys_sem.at[side], yr_sem.at[1 - side],
             device(0, -1 if side == 0 else 1),
         )
-
-    has = ((ix > 0, ix < nx - 1), (iy > 0, iy < ny - 1))
-    for side in range(2):
-        @pl.when(has[0][side])
-        def _():
-            for f in range(5):
-                xcopy(side, f).start()
-
-        @pl.when(has[1][side])
-        def _():
-            ycopy(side).start()
 
     zmask = lax.broadcasted_iota(jnp.int32, (cy, nz), 1) < nz - 1
     ymask = lax.broadcasted_iota(jnp.int32, (cy, nz), 0) < cy - 1
@@ -226,7 +276,49 @@
         return tuple(fx)
 
     zero = jnp.zeros((cy, nz), jnp.float32)
-    lax.fori_loop(0, cx, slab, (zero, zero, zero), unroll=2)
+    quarter = cx // 4
+
+    def march(start, stop):
+        before = tuple(between[f] for f in range(3)) if start else (zero, zero, zero)
+        edge = lax.fori_loop(start, stop, slab, before, unroll=2)
+        if stop < cx:
+            for f in range(3):
+                between[f] = edge[f]
+
+    march(0, quarter)
+
+    def onward(j, dy):
+        slot, dev = 3 * j + dy + 1, (nx - 1, wrap(iy - 1 + j))
+        return (
+            remote(via_i.at[slot], idx_s.at[dy + 1], ws_sem.at[0], ir_sem.at[0], dev),
+            remote(via_f.at[slot], recv.at[dy + 1], ws_sem.at[1], fr_sem.at[0], dev),
+        )
+
+    @pl.when(relays)
+    def _():
+        for j in (0, 1):
+            pl.semaphore_wait(go_sem.at[j], 1)
+            arrived(via_i.at[pl.ds(3 * j, 3)], vi_sem.at[j])
+            arrived(via_f.at[pl.ds(3 * j, 3)], vf_sem.at[j])
+            for dy in (-1, 0, 1):
+                for c in onward(j, dy):
+                    c.start()
+
+    march(quarter, 2 * quarter)
+    has = ((ix > 0, ix < nx - 1), (iy > 0, iy < ny - 1))
+    for side in range(2):
+        @pl.when(has[0][side])
+        def _():
+            for f in range(5):
+                xcopy(side, f).start()
+
+        @pl.when(has[1][side])
+        def _():
+            ycopy(side).start()
+
+    @pl.when(~last)
+    def _():
+        march(2 * quarter, cx)
 
     def answer(group, sources):
         first = 3 * group
@@ -264,7 +356,7 @@
         n = 3 * (dx + 1) + dy + 1
         return remote(back.at[n], ret.at[n], bs_sem, br_sem, device(-dx, -dy))
 
-    for dx in (0, away, -away):
+    def serve(dx):
         group = dx + 1
         still = isinstance(dx, int)
         many = 2 if still else 3
@@ -272,8 +364,28 @@
         answer(group, (idx_s, own_s, idx_s) if still else (idx_s,) * 3)
         arrived(recv.at[pl.ds(3 * group, many)], fr_sem.at[group])
         flows_of(group)
+        if not still:
+            @pl.when(first & (dx == 1))
+            def _():
+                pl.semaphore_wait(here_sem, 3)
+
         for dy in (-1, 1) if still else (-1, 1, 0):
             reply(dx, dy).start()
+
+    @pl.when(last)
+    def _():
+        serve(-away)
+
+    serve(0)
+    serve(away)
+
+    @pl.when(~last)
+    def _():
+        serve(-away)
+
+    @pl.when(last)
+    def _():
+        march(2 * quarter, cx)
 
     for side in range(2):
         @pl.when(has[0][side])
@@ -334,6 +446,11 @@
     for n in OTHERS:
         for r in range(CAP):
             scl[n, r : r + 1, :] = v[pl.ds(own_s[n, 0, 3 * CAP + r], 1), :]
+    @pl.when(relays)
+    def _():
+        arrived(via_i, ws_sem.at[0])
+        arrived(via_f, ws_sem.at[1])
+
     arrived(idx_send.at[pl.ds(0, 8)], is_sem)
     arrived(send.at[pl.ds(0, 8)], fs_sem)
     arrived(back.at[pl.ds(0, 8)], bs_sem)
@@ -364,6 +481,7 @@
     cells = cx * cy
     f32 = jnp.float32
     dma = pltpu.SemaphoreType.DMA
+    regular = pltpu.SemaphoreType.REGULAR
     any_spec = pl.BlockSpec(memory_space=pltpu.HBM)
     vmem = pl.BlockSpec(memory_space=pltpu.VMEM)
     smem = pl.BlockSpec(memory_space=pltpu.SMEM)
@@ -398,6 +516,10 @@
             dma((7,)), dma,
             dma, dma((3,)), dma, dma((3,)), dma, dma,
             dma((2,)), dma((2,)), dma((2,)), dma((2,)),
+            pltpu.VMEM((3, cy, nz), f32),
+            pltpu.VMEM((6, 1, 128), jnp.int32),
+            pltpu.VMEM((6, ROWS, 2 * nz), f32),
+            dma((2,)), dma((2,)), dma((2,)), regular((2,)), regular,
         ],
         compiler_params=pltpu.CompilerParams(
             collective_id=0, has_side_effects=True, vmem_limit_bytes=60000000

time: 17.5 us -> 16.3 us (0.931)
  Pallas kernels: 16.7 us -> 15.4 us
    pallas_call x1, Pallas kernels: 15.4 us -> 14.1 us  [body(): pl.pallas_call(functools.partial(kernel, cx, cy, nz, nrow), out_shape=(pl...]
where the time goes in v2:
time: 16.3 us; the launch traced here: 16.1 us
  Pallas kernels  15.4 us (94%)
  between operations  0.66 us (4%)
    pallas_call x1, Pallas kernels, body(): pl.pallas_call(functools.partial(kernel, cx, cy, nz, nrow), out_shape=(pl...  14.1 us
    pallas_call x1, Pallas kernels, body(): pl.pallas_call(functools.partial(finish, cells, nz), out_shape=(pltpu.VME...  1.29 us

profile of v2, /device:TPU:0, one launch (start us, length us, event | category | flops | bytes accessed | tf_op | source)
XLA Modules:
  0.0 16.1 jit_solution(5994038099562196470)
XLA Ops:
  0.7 14.1 %shard_map.91 = (f32[3072,128]{1,0:T(8,128)S(1)}, f32[9,4,384]{2,1,0:T(4,128)S(1)}, s32[9,1,128]{2,1,0:T(1,128)S(4)}) custom-call(f32[1024,128]{1,0:T(8,128)} %bitcast.9, f32[1024,128]{1,0:T(8,128)} %bitcast.10, f32[2048,128]{1,0:T(8,128)} %bitcast.8, f32[3072,128]{1,0:T(8,128)} %bitcast.7, f32[1024,128]{1,0:T(8,128)} %bitcast.11, s32[3,32]{1,0:T(4,128)} %bitcast.12, ...), custom_call_target="tpu_custom_call" | custom-call | tf_op jit(solution)/shard_map/pallas_call | solution.py:488
  14.8 1.3 %shard_map.92 = (f32[3072,128]{1,0:T(8,128)S(1)}, f32[9,4,384]{2,1,0:T(4,128)S(1)}, f32[3072,128]{1,0:T(8,128)}) custom-call(f32[3072,128]{1,0:T(8,128)S(1)} %get-tuple-element.9.part, f32[9,4,384]{2,1,0:T(4,128)S(1)} %get-tuple-element.10.res_in, s32[9,1,128]{2,1,0:T(1,128)S(4)} %get-tuple-element.11.own_s), custom_call_target="tpu_custom_call", output_to_operand_aliasing={{0}: (0, {}), {1}: (1, {})} | custom-call | tf_op jit(solution)/shard_map/pallas_call | solution.py:538

commit v3 on v1

v3 whole, which is shorter than its diff:
```python
import functools

import jax
import jax.numpy as jnp
from jax import lax
from jax.experimental import pallas as pl
from jax.experimental.pallas import tpu as pltpu
from jax.sharding import PartitionSpec as P

CAP = 4
ROWS = 2 * CAP
VISCOSITY = (0.5, 1.0, 0.25)
DENSITY = (1.0, 0.8, 0.25)
STEP = 0.2
MESH = pl.DeviceIdType.MESH
NEAR = [(dx, dy) for dx in (-1, 0, 1) for dy in (-1, 0, 1)]
HOME = 4
OTHERS = [n for n in range(9) if n != HOME]
PIECES = 12


def mobility(w, o):
    g = 1.0 - w - o
    return (w * w * (1.0 / VISCOSITY[0]), o * o, g * g * (1.0 / VISCOSITY[2]))


def harmonic(a, b):
    return 2.0 * a * b / (a + b)


def flux(dp, dd, low, high, trans):
    flows = []
    for f in range(3):
        drive = dp - DENSITY[f] * dd if DENSITY[f] != 1.0 else dp - dd
        flows.append(trans * jnp.where(drive > 0.0, low[f], high[f]) * drive)
    return flows


def edge_flux(low, high):
    return flux(
        low[0] - high[0],
        low[1] - high[1],
        mobility(low[2], low[3]),
        mobility(high[2], high[3]),
        harmonic(low[4], high[4]),
    )


def kernel(
    cx, cy, nz, nrow,
    p_hbm, d_hbm, s_hbm, k_hbm, v_hbm, pairs_hbm, kind_hbm, count_hbm, table_hbm,
    out, res, own_s,
    cell, k, v, table, pairs_v, count_s, kindrow,
    idx_send, idx_s, send, recv, loc, tloc, back, ret, scl,
    xhalo, yhalo,
    ir_sem, fr_sem, br_sem, xr_sem, yr_sem,
    between, via_i, via_f, vi_sem, vf_sem, go_sem, here_sem,
):
    def arrived(ref, sem):
        pltpu.make_async_copy(ref, ref, sem).wait()

    def work(load_sem, own_sem, out_sem, ws_sem, xs_sem, ys_sem):
        nx = lax.axis_size("gx")
        ny = lax.axis_size("gy")
        ix = lax.axis_index("gx")
        iy = lax.axis_index("gy")
        cells = cx * cy
        p, d, s = (cell.at[pl.ds(i * cells, (1, 1, 2)[i] * cells)] for i in range(3))

        def device(dx, dy):
            return (lax.rem(ix + dx + nx, nx), lax.rem(iy + dy + ny, ny))

        def remote(src, dst, ss, rs, dev):
            return pltpu.make_async_remote_copy(
                src_ref=src, dst_ref=dst, send_sem=ss, recv_sem=rs, device_id=dev, device_id_type=MESH
            )

        def signal(sem, dev):
            pl.semaphore_signal(sem, inc=1, device_id=dev, device_id_type=MESH)

        def wrap(y):
            return lax.rem(y + 2 * ny, ny)

        first, last = ix == 0, ix == nx - 1
        y_odd = lax.rem(iy, 2)
        relays = (ix == 1) & (y_odd == 1)
        barrier = pltpu.get_barrier_semaphore()
        for n in OTHERS:
            dx, dy = NEAR[n]
            if dx == 1:
                @pl.when(ix < nx - 2)
                def _():
                    signal(barrier, device(dx, dy))
            elif dx == 0:
                @pl.when(~last)
                def _():
                    signal(barrier, device(dx, dy))
            else:
                signal(barrier, device(dx, dy))

        @pl.when(relays)
        def _():
            signal(barrier, (nx - 1, wrap(iy - 1)))
            signal(barrier, (nx - 1, iy))
            signal(barrier, (0, wrap(iy - 2)))

        loads = [
            pltpu.make_async_copy(src, dst, load_sem.at[i])
            for i, src, dst in (
                (0, pairs_hbm, pairs_v),
                (1, kind_hbm, kindrow),
                (2, count_hbm, count_s),
                (3, p_hbm, p),
                (3, d_hbm, d),
                (3, s_hbm, s),
                (4, k_hbm, k),
                (5, v_hbm, v),
                (6, table_hbm, table),
            )
        ]
        for c in loads:
            c.start()

        @pl.when(last)
        def _():
            pl.semaphore_wait(barrier, 4)
            signal(go_sem.at[y_odd], (1, iy + 1 - y_odd))
            for dy in (-1, 0, 1):
                signal(here_sem, (0, wrap(iy + dy)))

        for c in loads[:3]:
            c.wait()
        lane_of_row = lax.broadcasted_iota(jnp.int32, (nrow, nrow), 1)
        sub_of_row = lax.broadcasted_iota(jnp.int32, (nrow, nrow), 0)
        eye = lane_of_row == sub_of_row
        pv = pairs_v[...]
        tgt_row = pv[1:2, :]

        def to_sublanes(row):
            return jnp.sum(jnp.where(eye, row, 0), axis=1, keepdims=True)

        src_col = to_sublanes(pv[0:1, :])
        tgt_col = to_sublanes(tgt_row)
        land_col = to_sublanes(pv[2:3, :])
        kind_col = to_sublanes(kindrow[...].reshape(1, nrow))
        rank_col = jnp.sum(
            ((tgt_col == tgt_row) & (lane_of_row < sub_of_row)).astype(jnp.int32), axis=1, keepdims=True
        )
        live_col = (lax.broadcasted_iota(jnp.int32, (nrow, 1), 0) < count_s[0]).astype(jnp.int32)
        code_col = jnp.zeros_like(tgt_col)
        for n in range(9):
            hx, hy = device(*NEAR[n])
            code_col = jnp.where(tgt_col == hx * ny + hy, n, code_col)
        lanes = lax.broadcasted_iota(jnp.int32, (nrow, 128), 1)
        message = (
            jnp.where(lanes == rank_col, land_col, 0)
            + jnp.where(lanes == CAP + rank_col, kind_col, 0)
            + jnp.where(lanes == 2 * CAP + rank_col, live_col, 0)
            + jnp.where(lanes == 3 * CAP + rank_col, src_col, 0)
        )
        for n in range(9):
            idx_send[n] = jnp.sum(jnp.where(code_col == n, message, 0), axis=0, keepdims=True)

        own_copy = pltpu.make_async_copy(idx_send, own_s, own_sem)
        own_copy.start()
        arrived(cell, load_sem.at[3])
        own_copy.wait()
        for n in range(9):
            dst = recv if n == HOME else send
            for r in range(CAP):
                col = own_s[n, 0, 3 * CAP + r]
                dst[n, r : r + 1, :nz] = p[pl.ds(col, 1), :]
                dst[n, CAP + r : CAP + r + 1, :nz] = d[pl.ds(col, 1), :]
                dst[n, r : r + 1, nz:] = s[pl.ds(col, 1), :]
                dst[n, CAP + r : CAP + r + 1, nz:] = s[pl.ds(cells + col, 1), :]

        odd = lax.rem(ix, 2)
        away = 2 * odd - 1

        def ask(dx, dy):
            n = 3 * (dx + 1) + dy + 1
            dev = device(dx, dy)
            slot = inbox(dx, dy)
            remote(idx_send.at[n], idx_s.at[n], out_sem, ir_sem.at[slot], dev).start()
            remote(send.at[n], recv.at[n], out_sem, fr_sem.at[slot], dev).start()

        def inbox(dx, dy):
            if isinstance(dx, int):
                return dy + 1 if dx < 0 else 3 + dx
            return jnp.where(dx < 0, dy + 1, 3 + dx)

        def relay_slot(j, off):
            if isinstance(off, int):
                return (0, 1 + j, 3 + j, 5)[off + 2]
            return jnp.where(off == -2, 0, jnp.where(off == -1, 1 + j, jnp.where(off == 0, 3 + j, 5)))

        @pl.when(first)
        def _():
            pl.semaphore_wait(barrier, 5 + y_odd)
            for dy in (-1, 0, 1):
                ty = wrap(iy + dy)
                t_odd = lax.rem(ty, 2)
                off = t_odd - 1 - dy
                slot = relay_slot(t_odd, off)
                via = (1, ty + 1 - t_odd)
                remote(idx_send.at[dy + 1], via_i.at[slot], out_sem, vi_sem.at[off + 2], via).start()
                remote(send.at[dy + 1], via_f.at[slot], out_sem, vf_sem.at[off + 2], via).start()

        @pl.when(~first)
        def _():
            @pl.when(~last)
            def _():
                pl.semaphore_wait(barrier, 8)

            @pl.when(ix == nx - 2)
            def _():
                for dy in (-1, 0, 1):
                    signal(here_sem, device(1, dy))

            @pl.when(last)
            def _():
                pl.semaphore_wait(here_sem, 3)

            for dy in (-1, 1, 0):
                ask(away, dy)

        def near_asks():
            for dy in (-1, 1, 0):
                ask(-away, dy)
            for dy in (-1, 1):
                ask(0, dy)

        @pl.when(~first)
        def _():
            near_asks()

        for c in loads[6:]:
            c.wait()
        xparts = [(p, 0), (d, 0), (s, 0), (s, cells), (k, 0)]
        yparts = [(p, 0), (d, 0), (s, 0), (s, cx), (k, cx)]

        def xcopy(side, f):
            ref, base = xparts[f]
            at = base + (0 if side == 0 else cells - cy)
            return remote(
                ref.at[pl.ds(at, cy), :], xhalo.at[1 - side, f], xs_sem.at[side], xr_sem.at[1 - side],
                device(-1 if side == 0 else 1, 0),
            )

        for f in range(5):
            ref, base = yparts[f]
            base = base * cy if f >= 3 else base
            for side in range(2):
                off = base + (0 if side == 0 else cy - 1)
                yhalo[2 + side, f] = ref[pl.ds(off, cx, stride=cy), :]

        def ycopy(side):
            return remote(
                yhalo.at[2 + side], yhalo.at[1 - side], ys_sem.at[side], yr_sem.at[1 - side],
                device(0, -1 if side == 0 else 1),
            )

        zmask = lax.broadcasted_iota(jnp.int32, (cy, nz), 1) < nz - 1
        ymask = lax.broadcasted_iota(jnp.int32, (cy, nz), 0) < cy - 1

        def slab(a, carry):
            base = pl.multiple_of(a * cy, cy)
            after = pl.multiple_of(jnp.minimum(a + 1, cx - 1) * cy, cy)

            def at(ref, off):
                return ref[pl.ds(off, cy), :]

            p0, d0 = at(p, base), at(d, base)
            w0, o0 = at(s, base), at(s, cells + base)
            m0 = mobility(w0, o0)
            m1 = mobility(at(s, after), at(s, cells + after))
            tx = jnp.where(a < cx - 1, harmonic(at(k, base), at(k, after)), 0.0)
            fx = flux(p0 - at(p, after), d0 - at(d, after), m0, m1, tx)
            net = [fx[f] - carry[f] for f in range(3)]
            for axis, size, mask, offset in ((0, cy, ymask, cells), (1, nz, zmask, 2 * cells)):
                def up(x):
                    return pltpu.roll(x, size - 1, axis)

                kk = at(k, offset + base)
                t = jnp.where(mask, harmonic(kk, up(kk)), 0.0)
                fl = flux(p0 - up(p0), d0 - up(d0), m0, [up(m) for m in m0], t)
                net = [net[f] + (fl[f] - pltpu.roll(fl[f], 1, axis)) for f in range(3)]
            scale = STEP / at(v, base)
            v[pl.ds(base, cy), :] = scale
            now = (w0, o0, 1.0 - w0 - o0)
            for f in range(3):
                out[pl.ds(f * cells + base, cy), :] = now[f] - scale * net[f]
            return tuple(fx)

        zero = jnp.zeros((cy, nz), jnp.float32)
        quarter = cx // 4

        def march(start, stop):
            before = tuple(between[f] for f in range(3)) if start else (zero, zero, zero)
            edge = lax.fori_loop(start, stop, slab, before, unroll=2)
            if stop < cx:
                for f in range(3):
                    between[f] = edge[f]

        march(0, quarter)

        @pl.when(first)
        def _():
            near_asks()

        def take(off):
            start, many = ((0, 1), (1, 2), (3, 2), (5, 1))[off + 2]
            arrived(via_i.at[pl.ds(start, many)], vi_sem.at[off + 2])
            arrived(via_f.at[pl.ds(start, many)], vf_sem.at[off + 2])

        def onward(j, off):
            dy = j - 1 - off
            slot, dev = relay_slot(j, off), (nx - 1, wrap(iy - 1 + j))
            remote(via_i.at[slot], idx_s.at[dy + 1], ws_sem, ir_sem.at[dy + 1], dev).start()
            remote(via_f.at[slot], recv.at[dy + 1], ws_sem, fr_sem.at[dy + 1], dev).start()

        def pass_on(plan):
            for step in plan:
                if step in ("even", "odd"):
                    pl.semaphore_wait(go_sem.at[int(step == "odd")], 1)
                elif isinstance(step, int):
                    take(step)
                else:
                    onward(*step)

        @pl.when(relays & (iy == 1))
        def _():
            pass_on(["even", 0, (0, 0), -1, (0, -1), -2, (0, -2), "odd", (1, -1), (1, 0), 1, (1, 1)])

        @pl.when(relays & (iy != 1))
        def _():
            pass_on(["odd", 1, (1, 1), "even", -2, (0, -2), 0, (0, 0), (1, 0), -1, (0, -1), (1, -1)])

        march(quarter, 2 * quarter)
        has = ((ix > 0, ix < nx - 1), (iy > 0, iy < ny - 1))
        for side in range(2):
            @pl.when(has[0][side])
            def _():
                for f in range(5):
                    xcopy(side, f).start()

            @pl.when(has[1][side])
            def _():
                ycopy(side).start()

        @pl.when(~last)
        def _():
            march(2 * quarter, cx)

        def answer(n, ints):
            for r in range(CAP):
                land = ints[n, 0, r]
                kd = ints[n, 0, CAP + r]
                live = ints[n, 0, 2 * CAP + r].astype(jnp.float32)
                loc[n, r : r + 1, :nz] = p[pl.ds(land, 1), :]
                loc[n, CAP + r : CAP + r + 1, :nz] = d[pl.ds(land, 1), :]
                loc[n, r : r + 1, nz:] = s[pl.ds(land, 1), :]
                loc[n, CAP + r : CAP + r + 1, nz:] = s[pl.ds(cells + land, 1), :]
                tloc[n, r : r + 1, :] = table[pl.ds(kd, 1), :] * live

        def flows_of(start, many):
            rows = pl.ds(start, many)
            far, here = recv[rows], loc[rows]

            def second(x):
                return pltpu.roll(x, CAP, 1)

            gap = far[:, :, :nz] - here[:, :, :nz]
            fl = flux(
                gap,
                second(gap),
                mobility(far[:, :, nz:], second(far[:, :, nz:])),
                mobility(here[:, :, nz:], second(here[:, :, nz:])),
                tloc[rows],
            )
            for f in range(3):
                back[rows, :, f * nz : (f + 1) * nz] = fl[f][:, :CAP]

        def reply(dx, dy):
            n = 3 * (dx + 1) + dy + 1
            return remote(back.at[n], ret.at[n], out_sem, br_sem, device(-dx, -dy))

        def landed(buf, sem, dx):
            start = 3 * (dx + 1)
            if dx < 0:
                for i in range(3):
                    arrived(buf.at[i], sem.at[i])
            else:
                arrived(buf.at[pl.ds(start, 2 + dx)], sem.at[3 + dx])

        def serve(dx):
            start = 3 * (dx + 1)
            landed(idx_s, ir_sem, dx)
            for i in range(3):
                answer(start + i, own_s if start + i == HOME else idx_s)
            landed(recv, fr_sem, dx)
            flows_of(start, 3)
            if dx == 1:
                @pl.when(first)
                def _():
                    pl.semaphore_wait(here_sem, 3)

            for dy in (-1, 1, 0):
                if dx or dy:
                    reply(dx, dy).start()

        @pl.when(last)
        def _():
            side = jnp.where((iy == 0) | (iy == ny - 1), -1, 1)
            for dy in (side, 0, -side):
                n = dy + 1
                arrived(idx_s.at[n], ir_sem.at[n])
                answer(n, idx_s)
                arrived(recv.at[n], fr_sem.at[n])
                flows_of(n, 1)
                reply(-1, dy).start()

        serve(0)

        @pl.when(odd == 1)
        def _():
            serve(1)

        @pl.when(~last)
        def _():
            serve(-1)

        @pl.when(odd == 0)
        def _():
            serve(1)

        @pl.when(last)
        def _():
            march(2 * quarter, cx)

        for side in range(2):
            @pl.when(has[0][side])
            def _():
                arrived(xhalo.at[side], xs_sem.at[side])
                arrived(xhalo.at[side], xr_sem.at[side])
                at = 0 if side == 0 else cells - cy
                mine = [ref[pl.ds(base + at, cy), :] for ref, base in xparts]
                near = [xhalo[side, f] for f in range(5)]
                low, high = (near, mine) if side == 0 else (mine, near)
                fl = edge_flux(low, high)
                scale = v[pl.ds(at, cy), :]
                for f in range(3):
                    rows = pl.ds(f * cells + at, cy)
                    out[rows, :] = out[rows, :] + (scale * fl[f] if side == 0 else -scale * fl[f])

        for side in range(2):
            @pl.when(has[1][side])
            def _():
                ycopy(side).wait_send()
                ycopy(1 - side).wait_recv()
                at = 0 if side == 0 else cy - 1
                mine = [yhalo[2 + side, f] for f in range(5)]
                near = [yhalo[side, f] for f in range(5)]
                low, high = (near, mine) if side == 0 else (mine, near)
                fl = edge_flux(low, high)
                scale = v[pl.ds(at, cx, stride=cy), :]
                for f in range(3):
                    rows = pl.ds(f * cells + at, cx, stride=cy)
                    out[rows, :] = out[rows, :] + (scale * fl[f] if side == 0 else -scale * fl[f])

        lane1 = lax.broadcasted_iota(jnp.int32, (1, 128), 1)
        slots = 10 * CAP
        spot = jnp.full((1, 128), -1, jnp.int32)
        for n in range(9):
            for r in range(CAP):
                spot = jnp.where(lane1 == n * CAP + r, (own_s if n == HOME else idx_s)[n, 0, r], spot)
        for r in range(CAP):
            spot = jnp.where(lane1 == 9 * CAP + r, own_s[HOME, 0, 3 * CAP + r], spot)
        spot = jnp.where(lane1 < slots, spot, 0)
        spot = spot + pltpu.roll(spot, slots, 1) + pltpu.roll(spot, 2 * slots, 1)
        flows = jnp.concatenate([-back[n] for n in range(9)] + [back[HOME]], axis=0)
        hi = flows.astype(jnp.bfloat16).astype(jnp.float32)
        rest = flows - hi
        mid = rest.astype(jnp.bfloat16).astype(jnp.float32)
        pad = jnp.zeros((128 - 3 * slots, 3 * nz), jnp.float32)
        parts = jnp.concatenate([hi, mid, rest - mid, pad], axis=0).astype(jnp.bfloat16)
        step = 8 * cy
        for c in range(cells // step):
            ids = lax.broadcasted_iota(jnp.int32, (step, 128), 0) + c * step
            hot = (ids == spot).astype(jnp.float32).astype(jnp.bfloat16)
            add = jnp.dot(hot, parts, preferred_element_type=jnp.float32)
            scale = v[c * step : (c + 1) * step, :]
            for f in range(3):
                at = pl.ds(f * cells + c * step, step)
                out[at, :] = out[at, :] - scale * add[:, f * nz : (f + 1) * nz]

        for n in OTHERS:
            for r in range(CAP):
                scl[n, r : r + 1, :] = v[pl.ds(own_s[n, 0, 3 * CAP + r], 1), :]
        @pl.when(relays)
        def _():
            arrived(cell.at[pl.ds(0, 6 * (1 + 2 * ROWS))], ws_sem)

        arrived(cell.at[pl.ds(0, 8 * (1 + 2 * ROWS + 3 * CAP))], out_sem)
    dma = pltpu.SemaphoreType.DMA
    pl.run_scoped(work, dma((7,)), dma, dma, dma, dma((2,)), dma((2,)))
    arrived(ret.at[pl.ds(0, 8)], br_sem)
    for n in OTHERS:
        for f in range(3):
            res[n, :, f * nz : (f + 1) * nz] = ret[n, :, f * nz : (f + 1) * nz] * scl[n]


def finish(cells, nz, part, res_in, own_s, held, res, final, sem):
    for n in OTHERS:
        for r in range(CAP):
            col = own_s[n, 0, 3 * CAP + r]
            for f in range(3):
                row = pl.ds(f * cells + col, 1)
                held[row, :] = held[row, :] - res[n, r : r + 1, f * nz : (f + 1) * nz]
    size = 3 * cells // PIECES
    for i in range(PIECES):
        rows = pl.ds(i * size, size)
        pltpu.make_async_copy(held.at[rows], final.at[rows], sem).start()
    pltpu.make_async_copy(held, final, sem).wait()


def body(pressure, depth, saturation, permeability, pore_volume, pairs, kind, count, table):
    cx, cy, nz = pressure.shape
    nrow = pairs.shape[0]
    kinds = table.shape[0]
    cells = cx * cy
    f32 = jnp.float32
    dma = pltpu.SemaphoreType.DMA
    regular = pltpu.SemaphoreType.REGULAR
    any_spec = pl.BlockSpec(memory_space=pltpu.HBM)
    vmem = pl.BlockSpec(memory_space=pltpu.VMEM)
    smem = pl.BlockSpec(memory_space=pltpu.SMEM)
    part, res, own = pl.pallas_call(
        functools.partial(kernel, cx, cy, nz, nrow),
        out_shape=(
            pltpu.VMEM((3 * cells, nz), f32),
            pltpu.VMEM((9, CAP, 3 * nz), f32),
            pltpu.SMEM((9, 1, 128), jnp.int32),
        ),
        in_specs=[any_spec] * 9,
        out_specs=(vmem, vmem, smem),
        scratch_shapes=[
            pltpu.VMEM((4 * cells, nz), f32),
            pltpu.VMEM((3 * cells, nz), f32),
            pltpu.VMEM((cells, nz), f32),
            pltpu.VMEM((kinds, nz), f32),
            pltpu.VMEM((3, nrow), jnp.int32),
            pltpu.SMEM((1,), jnp.int32),
            pltpu.VMEM((nrow,), jnp.int32),
            pltpu.VMEM((9, 1, 128), jnp.int32),
            pltpu.SMEM((9, 1, 128), jnp.int32),
            pltpu.VMEM((9, ROWS, 2 * nz), f32),
            pltpu.VMEM((9, ROWS, 2 * nz), f32),
            pltpu.VMEM((9, ROWS, 2 * nz), f32),
            pltpu.VMEM((9, ROWS, nz), f32),
            pltpu.VMEM((9, CAP, 3 * nz), f32),
            pltpu.VMEM((9, CAP, 3 * nz), f32),
            pltpu.VMEM((9, CAP, nz), f32),
            pltpu.VMEM((2, 5, cy, nz), f32),
            pltpu.VMEM((4, 5, cx, nz), f32),
            dma((5,)), dma((5,)), dma, dma((2,)), dma((2,)),
            pltpu.VMEM((3, cy, nz), f32),
            pltpu.VMEM((6, 1, 128), jnp.int32),
            pltpu.VMEM((6, ROWS, 2 * nz), f32),
            dma((4,)), dma((4,)), regular((2,)), regular,
        ],
        compiler_params=pltpu.CompilerParams(
            collective_id=0, has_side_effects=True, vmem_limit_bytes=60000000
        ),
    )(
        pressure.reshape(cells, nz),
        depth.reshape(cells, nz),
        saturation.reshape(2 * cells, nz),
        permeability.reshape(3 * cells, nz),
        pore_volume.reshape(cells, nz),
        pairs.T,
        kind,
        count,
        table,
    )
    _, _, out = pl.pallas_call(
        functools.partial(finish, cells, nz),
        out_shape=(
            pltpu.VMEM((3 * cells, nz), f32),
            pltpu.VMEM((9, CAP, 3 * nz), f32),
            jax.ShapeDtypeStruct((3 * cells, nz), f32),
        ),
        in_specs=[vmem, vmem, smem],
        out_specs=(vmem, vmem, any_spec),
        scratch_shapes=[dma],
        input_output_aliases={0: 0, 1: 1},
    )(part, res, own)
    return out.reshape(3, cx, cy, nz)


def solution(mesh):
    cell = P("gx", "gy", None)
    cells = P(None, "gx", "gy", None)
    both = ("gx", "gy")
    return jax.shard_map(
        body,
        mesh=mesh,
        in_specs=(cell, cell, cells, cells, cell, P(both, None), P(both), P(both), P()),
        out_specs=cells,
        check_vma=False,
    )
```

time: 17.5 us -> 16 us (0.914)
  Pallas kernels: 16.7 us -> 15.1 us
    pallas_call x1, Pallas kernels: 15.4 us -> 13.8 us  [body(): pl.pallas_call(functools.partial(kernel, cx, cy, nz, nrow), out_shape=(pl...]
where the time goes in v3:
time: 16 us; the launch traced here: 15.8 us
  Pallas kernels  15.1 us (94%)
  between operations  0.66 us (4%)
    pallas_call x1, Pallas kernels, body(): pl.pallas_call(functools.partial(kernel, cx, cy, nz, nrow), out_shape=(pl...  13.8 us
    pallas_call x1, Pallas kernels, body(): pl.pallas_call(functools.partial(finish, cells, nz), out_shape=(pltpu.VME...  1.29 us

profile of v3, /device:TPU:0, one launch (start us, length us, event | category | flops | bytes accessed | tf_op | source)
XLA Modules:
  0.0 15.8 jit_solution(2903284048707598020)
XLA Ops:
  0.7 13.8 %shard_map.91 = (f32[3072,128]{1,0:T(8,128)S(1)}, f32[9,4,384]{2,1,0:T(4,128)S(1)}, s32[9,1,128]{2,1,0:T(1,128)S(4)}) custom-call(f32[1024,128]{1,0:T(8,128)} %bitcast.9, f32[1024,128]{1,0:T(8,128)} %bitcast.10, f32[2048,128]{1,0:T(8,128)} %bitcast.8, f32[3072,128]{1,0:T(8,128)} %bitcast.7, f32[1024,128]{1,0:T(8,128)} %bitcast.11, s32[3,32]{1,0:T(4,128)} %bitcast.12, ...), custom_call_target="tpu_custom_call" | custom-call | tf_op jit(solution)/shard_map/pallas_call | solution.py:538
  14.5 1.3 %shard_map.92 = (f32[3072,128]{1,0:T(8,128)S(1)}, f32[9,4,384]{2,1,0:T(4,128)S(1)}, f32[3072,128]{1,0:T(8,128)}) custom-call(f32[3072,128]{1,0:T(8,128)S(1)} %get-tuple-element.9.part, f32[9,4,384]{2,1,0:T(4,128)S(1)} %get-tuple-element.10.res_in, s32[9,1,128]{2,1,0:T(1,128)S(4)} %get-tuple-element.11.own_s), custom_call_target="tpu_custom_call", output_to_operand_aliasing={{0}: (0, {}), {1}: (1, {})} | custom-call | tf_op jit(solution)/shard_map/pallas_call | solution.py:586

commit v4 on v3

--- a/solution.py
+++ b/solution.py
@@ -13,8 +13,8 @@
 DENSITY = (1.0, 0.8, 0.25)
 STEP = 0.2
 MESH = pl.DeviceIdType.MESH
-NEAR = [(dx, dy) for dx in (-1, 0, 1) for dy in (-1, 0, 1)]
-HOME = 4
+NEAR = [(dx, dy) for dx in (-1, 0, 1) for dy in ((-1, 1, 0) if dx == 0 else (-1, 0, 1))]
+HOME = 5
 OTHERS = [n for n in range(9) if n != HOME]
 PIECES = 12
 
@@ -54,10 +54,13 @@
     idx_send, idx_s, send, recv, loc, tloc, back, ret, scl,
     xhalo, yhalo,
     ir_sem, fr_sem, br_sem, xr_sem, yr_sem,
-    between, via_i, via_f, vi_sem, vf_sem, go_sem, here_sem,
+    between, via_i, via_f, vi_sem, vf_sem, go_sem, here_sem, near_sem,
 ):
     def arrived(ref, sem):
         pltpu.make_async_copy(ref, ref, sem).wait()
+
+    def seat(n):
+        return n - 1 if isinstance(n, int) and n > HOME else n
 
     def work(load_sem, own_sem, out_sem, ws_sem, xs_sem, ys_sem):
         nx = lax.axis_size("gx")
@@ -92,17 +95,28 @@
                 def _():
                     signal(barrier, device(dx, dy))
             elif dx == 0:
-                @pl.when(~last)
+                @pl.when(~first & ~last)
                 def _():
                     signal(barrier, device(dx, dy))
             else:
-                signal(barrier, device(dx, dy))
+                @pl.when((ix > 1) | relays)
+                def _():
+                    signal(barrier, device(dx, dy))
+
+        @pl.when(first & (y_odd == 1))
+        def _():
+            signal(barrier, (1, wrap(iy + 2)))
 
         @pl.when(relays)
         def _():
             signal(barrier, (nx - 1, wrap(iy - 1)))
             signal(barrier, (nx - 1, iy))
             signal(barrier, (0, wrap(iy - 2)))
+
+        @pl.when(last)
+        def _():
+            pl.semaphore_wait(barrier, 1)
+            signal(go_sem.at[y_odd], (1, iy + 1 - y_odd))
 
         loads = [
             pltpu.make_async_copy(src, dst, load_sem.at[i])
@@ -120,13 +134,6 @@
         ]
         for c in loads:
             c.start()
-
-        @pl.when(last)
-        def _():
-            pl.semaphore_wait(barrier, 4)
-            signal(go_sem.at[y_odd], (1, iy + 1 - y_odd))
-            for dy in (-1, 0, 1):
-                signal(here_sem, (0, wrap(iy + dy)))
 
         for c in loads[:3]:
             c.wait()
@@ -177,8 +184,13 @@
         odd = lax.rem(ix, 2)
         away = 2 * odd - 1
 
+        def place(dx, dy):
+            if isinstance(dx, int) and dx == 0:
+                return NEAR.index((0, dy))
+            return 3 * (dx + 1) + dy + 1
+
         def ask(dx, dy):
-            n = 3 * (dx + 1) + dy + 1
+            n = place(dx, dy)
             dev = device(dx, dy)
             slot = inbox(dx, dy)
             remote(idx_send.at[n], idx_s.at[n], out_sem, ir_sem.at[slot], dev).start()
@@ -194,9 +206,19 @@
                 return (0, 1 + j, 3 + j, 5)[off + 2]
             return jnp.where(off == -2, 0, jnp.where(off == -1, 1 + j, jnp.where(off == 0, 3 + j, 5)))
 
+        def far_asks():
+            for dy in (-1, 1, 0):
+                ask(away, dy)
+
+        def near_asks():
+            for dy in (-1, 1, 0):
+                ask(-away, dy)
+            for dy in (-1, 1):
+                ask(0, dy)
+
         @pl.when(first)
         def _():
-            pl.semaphore_wait(barrier, 5 + y_odd)
+            pl.semaphore_wait(barrier, 2)
             for dy in (-1, 0, 1):
                 ty = wrap(iy + dy)
                 t_odd = lax.rem(ty, 2)
@@ -210,7 +232,14 @@
         def _():
             @pl.when(~last)
             def _():
-                pl.semaphore_wait(barrier, 8)
+                pl.semaphore_wait(barrier, 8 + relays.astype(jnp.int32))
+
+            @pl.when(relays)
+            def _():
+                signal(barrier, (nx - 1, wrap(iy - 1)))
+                signal(barrier, (nx - 1, iy))
+                for off in (-2, -1, 0, 1):
+                    signal(near_sem, (0, wrap(iy + off)))
 
             @pl.when(ix == nx - 2)
             def _():
@@ -219,18 +248,16 @@
 
             @pl.when(last)
             def _():
+                pl.semaphore_wait(barrier, 1)
+                for dy in (-1, 0, 1):
+                    signal(here_sem, device(1, dy))
                 pl.semaphore_wait(here_sem, 3)
 
-            for dy in (-1, 1, 0):
-                ask(away, dy)
-
-        def near_asks():
-            for dy in (-1, 1, 0):
-                ask(-away, dy)
-            for dy in (-1, 1):
-                ask(0, dy)
-
-        @pl.when(~first)
+            @pl.when(ix != 2)
+            def _():
+                far_asks()
+
+        @pl.when(~first & (ix != 2))
         def _():
             near_asks()
 
@@ -304,7 +331,15 @@
 
         march(0, quarter)
 
+        @pl.when(ix == 2)
+        def _():
+            far_asks()
+
         @pl.when(first)
+        def _():
+            pl.semaphore_wait(near_sem, 2)
+
+        @pl.when(first | (ix == 2))
         def _():
             near_asks()
 
@@ -330,11 +365,11 @@
 
         @pl.when(relays & (iy == 1))
         def _():
-            pass_on(["even", 0, (0, 0), -1, (0, -1), -2, (0, -2), "odd", (1, -1), (1, 0), 1, (1, 1)])
+            pass_on(["odd", "even", 0, (0, 0), (1, 0), -1, (0, -1), (1, -1), -2, (0, -2), 1, (1, 1)])
 
         @pl.when(relays & (iy != 1))
         def _():
-            pass_on(["odd", 1, (1, 1), "even", -2, (0, -2), 0, (0, 0), (1, 0), -1, (0, -1), (1, -1)])
+            pass_on(["even", -2, (0, -2), "odd", 1, (1, 1), 0, (0, 0), (1, 0), -1, (0, -1), (1, -1)])
 
         march(quarter, 2 * quarter)
         has = ((ix > 0, ix < nx - 1), (iy > 0, iy < ny - 1))
@@ -382,8 +417,8 @@
                 back[rows, :, f * nz : (f + 1) * nz] = fl[f][:, :CAP]
 
         def reply(dx, dy):
-            n = 3 * (dx + 1) + dy + 1
-            return remote(back.at[n], ret.at[n], out_sem, br_sem, device(-dx, -dy))
+            n = place(dx, dy)
+            return remote(back.at[n], ret.at[seat(n)], out_sem, br_sem, device(-dx, -dy))
 
         def landed(buf, sem, dx):
             start = 3 * (dx + 1)
@@ -504,10 +539,10 @@
         arrived(cell.at[pl.ds(0, 8 * (1 + 2 * ROWS + 3 * CAP))], out_sem)
     dma = pltpu.SemaphoreType.DMA
     pl.run_scoped(work, dma((7,)), dma, dma, dma, dma((2,)), dma((2,)))
-    arrived(ret.at[pl.ds(0, 8)], br_sem)
+    arrived(ret, br_sem)
     for n in OTHERS:
         for f in range(3):
-            res[n, :, f * nz : (f + 1) * nz] = ret[n, :, f * nz : (f + 1) * nz] * scl[n]
+            res[n, :, f * nz : (f + 1) * nz] = ret[seat(n), :, f * nz : (f + 1) * nz] * scl[n]
 
 
 def finish(cells, nz, part, res_in, own_s, held, res, final, sem):
@@ -559,7 +594,7 @@
             pltpu.VMEM((9, ROWS, 2 * nz), f32),
             pltpu.VMEM((9, ROWS, nz), f32),
             pltpu.VMEM((9, CAP, 3 * nz), f32),
-            pltpu.VMEM((9, CAP, 3 * nz), f32),
+            pltpu.VMEM((8, CAP, 3 * nz), f32),
             pltpu.VMEM((9, CAP, nz), f32),
             pltpu.VMEM((2, 5, cy, nz), f32),
             pltpu.VMEM((4, 5, cx, nz), f32),
@@ -567,7 +602,7 @@
             pltpu.VMEM((3, cy, nz), f32),
             pltpu.VMEM((6, 1, 128), jnp.int32),
             pltpu.VMEM((6, ROWS, 2 * nz), f32),
-            dma((4,)), dma((4,)), regular((2,)), regular,
+            dma((4,)), dma((4,)), regular((2,)), regular, regular,
         ],
         compiler_params=pltpu.CompilerParams(
             collective_id=0, has_side_effects=True, vmem_limit_bytes=60000000

time: 16 us -> 15.7 us (0.981)
  Pallas kernels: 15.1 us -> 14.9 us
    pallas_call x1, Pallas kernels: 13.8 us -> 13.6 us  [body(): pl.pallas_call(functools.partial(kernel, cx, cy, nz, nrow), out_shape=(pl...]
where the time goes in v4:
time: 15.7 us; the launch traced here: 15.5 us
  Pallas kernels  14.9 us (95%)
  between operations  0.66 us (4%)
    pallas_call x1, Pallas kernels, body(): pl.pallas_call(functools.partial(kernel, cx, cy, nz, nrow), out_shape=(pl...  13.6 us
    pallas_call x1, Pallas kernels, body(): pl.pallas_call(functools.partial(finish, cells, nz), out_shape=(pltpu.VME...  1.29 us

profile of v4, /device:TPU:0, one launch (start us, length us, event | category | flops | bytes accessed | tf_op | source)
XLA Modules:
  0.0 15.5 jit_solution(18193212688463771273)
XLA Ops:
  0.7 13.6 %shard_map.91 = (f32[3072,128]{1,0:T(8,128)S(1)}, f32[9,4,384]{2,1,0:T(4,128)S(1)}, s32[9,1,128]{2,1,0:T(1,128)S(4)}) custom-call(f32[1024,128]{1,0:T(8,128)} %bitcast.9, f32[1024,128]{1,0:T(8,128)} %bitcast.10, f32[2048,128]{1,0:T(8,128)} %bitcast.8, f32[3072,128]{1,0:T(8,128)} %bitcast.7, f32[1024,128]{1,0:T(8,128)} %bitcast.11, s32[3,32]{1,0:T(4,128)} %bitcast.12, ...), custom_call_target="tpu_custom_call" | custom-call | tf_op jit(solution)/shard_map/pallas_call | solution.py:573
  14.2 1.3 %shard_map.92 = (f32[3072,128]{1,0:T(8,128)S(1)}, f32[9,4,384]{2,1,0:T(4,128)S(1)}, f32[3072,128]{1,0:T(8,128)}) custom-call(f32[3072,128]{1,0:T(8,128)S(1)} %get-tuple-element.9.part, f32[9,4,384]{2,1,0:T(4,128)S(1)} %get-tuple-element.10.res_in, s32[9,1,128]{2,1,0:T(1,128)S(4)} %get-tuple-element.11.own_s), custom_call_target="tpu_custom_call", output_to_operand_aliasing={{0}: (0, {}), {1}: (1, {})} | custom-call | tf_op jit(solution)/shard_map/pallas_call | solution.py:621

commit v5 on v4

--- a/solution.py
+++ b/solution.py
@@ -219,7 +219,7 @@
         @pl.when(first)
         def _():
             pl.semaphore_wait(barrier, 2)
-            for dy in (-1, 0, 1):
+            for dy in (y_odd, 1 - 2 * y_odd, y_odd - 1):
                 ty = wrap(iy + dy)
                 t_odd = lax.rem(ty, 2)
                 off = t_odd - 1 - dy

time: 15.7 us -> 15.6 us (level)
  no operation moved by 1% of the time
where the time goes in v5:
time: 15.6 us; the launch traced here: 15.4 us
  Pallas kernels  14.8 us (95%)
  between operations  0.66 us (4%)
    pallas_call x1, Pallas kernels, body(): pl.pallas_call(functools.partial(kernel, cx, cy, nz, nrow), out_shape=(pl...  13.5 us
    pallas_call x1, Pallas kernels, body(): pl.pallas_call(functools.partial(finish, cells, nz), out_shape=(pltpu.VME...  1.3 us

profile of v5, /device:TPU:0, one launch (start us, length us, event | category | flops | bytes accessed | tf_op | source)
XLA Modules:
  0.0 15.4 jit_solution(16225886308812691551)
XLA Ops:
  0.7 13.5 %shard_map.91 = (f32[3072,128]{1,0:T(8,128)S(1)}, f32[9,4,384]{2,1,0:T(4,128)S(1)}, s32[9,1,128]{2,1,0:T(1,128)S(4)}) custom-call(f32[1024,128]{1,0:T(8,128)} %bitcast.9, f32[1024,128]{1,0:T(8,128)} %bitcast.10, f32[2048,128]{1,0:T(8,128)} %bitcast.8, f32[3072,128]{1,0:T(8,128)} %bitcast.7, f32[1024,128]{1,0:T(8,128)} %bitcast.11, s32[3,32]{1,0:T(4,128)} %bitcast.12, ...), custom_call_target="tpu_custom_call" | custom-call | tf_op jit(solution)/shard_map/pallas_call | solution.py:573
  14.1 1.3 %shard_map.92 = (f32[3072,128]{1,0:T(8,128)S(1)}, f32[9,4,384]{2,1,0:T(4,128)S(1)}, f32[3072,128]{1,0:T(8,128)}) custom-call(f32[3072,128]{1,0:T(8,128)S(1)} %get-tuple-element.9.part, f32[9,4,384]{2,1,0:T(4,128)S(1)} %get-tuple-element.10.res_in, s32[9,1,128]{2,1,0:T(1,128)S(4)} %get-tuple-element.11.own_s), custom_call_target="tpu_custom_call", output_to_operand_aliasing={{0}: (0, {}), {1}: (1, {})} | custom-call | tf_op jit(solution)/shard_map/pallas_call | solution.py:621

commit v6 on v5

--- a/solution.py
+++ b/solution.py
@@ -88,6 +88,17 @@
         y_odd = lax.rem(iy, 2)
         relays = (ix == 1) & (y_odd == 1)
         barrier = pltpu.get_barrier_semaphore()
+        @pl.when(relays)
+        def _():
+            signal(barrier, (nx - 1, wrap(iy - 1)))
+            signal(barrier, (nx - 1, iy))
+            signal(barrier, (0, wrap(iy - 2)))
+
+        @pl.when(last)
+        def _():
+            pl.semaphore_wait(barrier, 1)
+            signal(go_sem.at[y_odd], (1, iy + 1 - y_odd))
+
         for n in OTHERS:
             dx, dy = NEAR[n]
             if dx == 1:
@@ -106,17 +117,6 @@
         @pl.when(first & (y_odd == 1))
         def _():
             signal(barrier, (1, wrap(iy + 2)))
-
-        @pl.when(relays)
-        def _():
-            signal(barrier, (nx - 1, wrap(iy - 1)))
-            signal(barrier, (nx - 1, iy))
-            signal(barrier, (0, wrap(iy - 2)))
-
-        @pl.when(last)
-        def _():
-            pl.semaphore_wait(barrier, 1)
-            signal(go_sem.at[y_odd], (1, iy + 1 - y_odd))
 
         loads = [
             pltpu.make_async_copy(src, dst, load_sem.at[i])

time: 15.6 us -> 15.6 us (level)
  no operation moved by 1% of the time
where the time goes in v6:
time: 15.6 us; the launch traced here: 15.5 us
  Pallas kernels  14.8 us (95%)
  between operations  0.66 us (4%)
    pallas_call x1, Pallas kernels, body(): pl.pallas_call(functools.partial(kernel, cx, cy, nz, nrow), out_shape=(pl...  13.5 us
    pallas_call x1, Pallas kernels, body(): pl.pallas_call(functools.partial(finish, cells, nz), out_shape=(pltpu.VME...  1.29 us

profile of v6, /device:TPU:0, one launch (start us, length us, event | category | flops | bytes accessed | tf_op | source)
XLA Modules:
  0.0 15.5 jit_solution(9929067364045609670)
XLA Ops:
  0.7 13.5 %shard_map.91 = (f32[3072,128]{1,0:T(8,128)S(1)}, f32[9,4,384]{2,1,0:T(4,128)S(1)}, s32[9,1,128]{2,1,0:T(1,128)S(4)}) custom-call(f32[1024,128]{1,0:T(8,128)} %bitcast.9, f32[1024,128]{1,0:T(8,128)} %bitcast.10, f32[2048,128]{1,0:T(8,128)} %bitcast.8, f32[3072,128]{1,0:T(8,128)} %bitcast.7, f32[1024,128]{1,0:T(8,128)} %bitcast.11, s32[3,32]{1,0:T(4,128)} %bitcast.12, ...), custom_call_target="tpu_custom_call" | custom-call | tf_op jit(solution)/shard_map/pallas_call | solution.py:573
  14.2 1.3 %shard_map.92 = (f32[3072,128]{1,0:T(8,128)S(1)}, f32[9,4,384]{2,1,0:T(4,128)S(1)}, f32[3072,128]{1,0:T(8,128)}) custom-call(f32[3072,128]{1,0:T(8,128)S(1)} %get-tuple-element.9.part, f32[9,4,384]{2,1,0:T(4,128)S(1)} %get-tuple-element.10.res_in, s32[9,1,128]{2,1,0:T(1,128)S(4)} %get-tuple-element.11.own_s), custom_call_target="tpu_custom_call", output_to_operand_aliasing={{0}: (0, {}), {1}: (1, {})} | custom-call | tf_op jit(solution)/shard_map/pallas_call | solution.py:621

commit v7 on v5

--- a/solution.py
+++ b/solution.py
@@ -16,7 +16,7 @@
 NEAR = [(dx, dy) for dx in (-1, 0, 1) for dy in ((-1, 1, 0) if dx == 0 else (-1, 0, 1))]
 HOME = 5
 OTHERS = [n for n in range(9) if n != HOME]
-PIECES = 12
+PIECES = 24
 
 
 def mobility(w, o):

time: 15.6 us -> 15.6 us (level)
  no operation moved by 1% of the time
where the time goes in v7:
time: 15.6 us; the launch traced here: 15.4 us
  Pallas kernels  14.8 us (95%)
  between operations  0.66 us (4%)
    pallas_call x1, Pallas kernels, body(): pl.pallas_call(functools.partial(kernel, cx, cy, nz, nrow), out_shape=(pl...  13.5 us
    pallas_call x1, Pallas kernels, body(): pl.pallas_call(functools.partial(finish, cells, nz), out_shape=(pltpu.VME...  1.29 us

profile of v7, /device:TPU:0, one launch (start us, length us, event | category | flops | bytes accessed | tf_op | source)
XLA Modules:
  0.0 15.4 jit_solution(14208520016622285656)
XLA Ops:
  0.7 13.5 %shard_map.91 = (f32[3072,128]{1,0:T(8,128)S(1)}, f32[9,4,384]{2,1,0:T(4,128)S(1)}, s32[9,1,128]{2,1,0:T(1,128)S(4)}) custom-call(f32[1024,128]{1,0:T(8,128)} %bitcast.9, f32[1024,128]{1,0:T(8,128)} %bitcast.10, f32[2048,128]{1,0:T(8,128)} %bitcast.8, f32[3072,128]{1,0:T(8,128)} %bitcast.7, f32[1024,128]{1,0:T(8,128)} %bitcast.11, s32[3,32]{1,0:T(4,128)} %bitcast.12, ...), custom_call_target="tpu_custom_call" | custom-call | tf_op jit(solution)/shard_map/pallas_call | solution.py:573
  14.1 1.3 %shard_map.92 = (f32[3072,128]{1,0:T(8,128)S(1)}, f32[9,4,384]{2,1,0:T(4,128)S(1)}, f32[3072,128]{1,0:T(8,128)}) custom-call(f32[3072,128]{1,0:T(8,128)S(1)} %get-tuple-element.9.part, f32[9,4,384]{2,1,0:T(4,128)S(1)} %get-tuple-element.10.res_in, s32[9,1,128]{2,1,0:T(1,128)S(4)} %get-tuple-element.11.own_s), custom_call_target="tpu_custom_call", output_to_operand_aliasing={{0}: (0, {}), {1}: (1, {})} | custom-call | tf_op jit(solution)/shard_map/pallas_call | solution.py:621
